TPU v7x, 128 devices: a whole 4x4x4 slice. The times are simulated.
128 devices in a mesh: row: 16 (over x, z), col: 8 (over y, core).
Axes of the slice: x: 4, y: 4, z: 4, core: 2. Of those that a mesh axis runs over, the one named last changes fastest.
Arguments:
- front_pivot: float32 [128, 128, 128], P('col', 'row'), may hold values from -256 to 256, as said below
- front_update: float32 [128, 640, 768], P('col', 'row'), may hold values from -12 to 12, as said below
- child_blocks: float32 [128, 2, 512, 512], P('col', None, 'row'), may hold values from -0.5 to 0.5, as said below
- child_map: int32 [128, 2, 512], P('col'), may hold values from -1 to 767, as said below
Outputs:
- lhat: float32 [128, 640, 128], P('col', 'row')
- schur: float32 [128, 640, 640], P('col', 'row')
- negative_share: float32 [], replicated
Inputs may be any that keep to these rules, and one draw needn't show every extreme that they name: `front_pivot`: symmetric in its last two dimensions. With both children's entries added, the pivot block of every front has an LDL^T factorization without pivoting whose pivots have magnitudes 4 to 40. `front_update`: the last 640 columns of each front form a symmetric matrix. `child_blocks`: symmetric in its last two dimensions. child_map[f, c, i] is the row and column of front f's assembled matrix that row and column i of child c go to, or -1 for padding. A child's entries of 0 or more are distinct, come before its padding, and number at least 385, and more than half of 512. Parent row p is held by grid row p // 8 if p < 128, else by (p - 128) // 40. Of the 32 rows i of a child with the same i // 32, at most 4 go to rows held by any one grid row, and every child reaches that bound.
All inputs are finite; a program needn't handle non-finite values.
Results may differ from a plain program's by a relative error of at most 0.0003.
Values sent between devices are 32-bit elements; how exact they have to be, the bound alone decides.
A program may use at most 64 MiB of HBM per device.

v0:
```python
import jax
import jax.numpy as jnp
from jax import lax
from jax.sharding import PartitionSpec as P

highest = lax.Precision.HIGHEST


def from_everyone(shard, axis):
    copies = jnp.broadcast_to(shard, (lax.axis_size(axis), *shard.shape))
    return lax.all_to_all(copies, axis, split_axis=0, concat_axis=0, tiled=True)


def joined_along(pieces, dim):
    lengths = list(pieces.shape[1:])
    lengths[dim] *= pieces.shape[0]
    return jnp.moveaxis(pieces, 0, dim).reshape(lengths)


def collect(shard, axis, dim):
    pieces = from_everyone(shard, axis)
    return joined_along(pieces, dim)


def taken_together(shard, axis):
    everything = from_everyone(shard, axis)
    return jnp.sum(everything, axis=0)


def factor(blocks):
    fronts, count = (blocks.shape[0], blocks.shape[-1])
    panel_width = 8
    index = jnp.arange(count, dtype=jnp.int32)

    def panel_step(panel, carry):
        current, lower, pivots = carry
        start = panel * panel_width
        strip = lax.dynamic_slice_in_dim(current, start, panel_width, 2)
        columns = []
        values = []
        for inner in range(panel_width):
            place = start + inner
            leading = lax.dynamic_index_in_dim(strip, place, 1, keepdims=False)
            pivot = leading[:, inner]
            below = index[None, :] > place
            column = strip[:, :, inner]
            multiplier = jnp.where(below, column / pivot[:, None], jnp.zeros_like(column))
            strip = strip - multiplier[:, :, None] * leading[:, None, :]
            columns.append(multiplier)
            values.append(pivot)
        panel_lower = jnp.stack(columns, axis=2)
        panel_pivots = jnp.stack(values, axis=1)
        lower = lax.dynamic_update_slice_in_dim(lower, panel_lower, start, 2)
        pivots = lax.dynamic_update_slice_in_dim(pivots, panel_pivots, start, 1)
        product = jnp.einsum(
            "fiw,fjw->fij", panel_lower * panel_pivots[:, None, :], panel_lower, precision=highest
        )
        later = index >= start + panel_width
        current = current - jnp.where(
            later[:, None] & later[None, :], product, jnp.zeros_like(product)
        )
        return (current, lower, pivots)

    start_state = (blocks, jnp.zeros_like(blocks), jnp.zeros((fronts, count), blocks.dtype))
    current, lower, pivots = lax.fori_loop(0, count // panel_width, panel_step, start_state)
    identity = jnp.eye(count, dtype=blocks.dtype)
    inverse = jax.vmap(
        lambda matrix: jax.scipy.linalg.solve_triangular(
            matrix, identity, lower=True, unit_diagonal=True
        )
    )(lower)
    return (inverse, pivots)


def local(front_pivot, front_update, child_blocks, child_map):
    row_count = lax.axis_size("row")
    my_row = lax.axis_index("row")
    fronts, pivot_rows, pivot_width = front_pivot.shape
    update_rows, width = (front_update.shape[1], front_update.shape[2])
    held, child_width = (child_blocks.shape[2], child_blocks.shape[3])
    capacity = 2 * held // row_count
    slot_count = row_count * capacity
    local_rows = pivot_rows + update_rows
    valid = child_map >= 0
    in_pivot = child_map < pivot_width
    owner = jnp.where(in_pivot, child_map // pivot_rows, (child_map - pivot_width) // update_rows)
    owner = jnp.where(valid, owner, row_count)
    target_row = jnp.where(
        in_pivot, child_map % pivot_rows, pivot_rows + (child_map - pivot_width) % update_rows
    )
    owner_hot = (owner[..., None] == jnp.arange(row_count, dtype=jnp.int32)).astype(jnp.int32)
    blocked = owner_hot.reshape(fronts, 2, row_count, held, row_count)
    earlier = jnp.cumsum(blocked, axis=3) - blocked
    rank = jnp.sum(earlier * blocked, axis=4).reshape(fronts, 2, child_width)
    position = jnp.arange(child_width, dtype=jnp.int32)
    slot = owner * capacity + rank
    arrival = (position // held)[None, None, :] * capacity + rank
    my_slot = lax.dynamic_slice_in_dim(slot, my_row * held, held, 2)
    my_valid = lax.dynamic_slice_in_dim(valid, my_row * held, held, 2)
    slot_range = jnp.arange(slot_count, dtype=jnp.int32)
    packing = (
        (my_slot[:, :, None, :] == slot_range[None, None, :, None]) & my_valid[:, :, None, :]
    ).astype(jnp.float32)
    outgoing = jnp.einsum("fcsq,fcqj->fcsj", packing, child_blocks, precision=highest)
    outgoing = outgoing.reshape(fronts, 2, row_count, capacity, child_width)
    incoming = lax.all_to_all(outgoing, "row", split_axis=2, concat_axis=2, tiled=True)
    incoming = incoming.reshape(fronts, 2, slot_count, child_width)
    mine = valid & (owner == my_row)
    row_hot = (
        (target_row[..., None] == jnp.arange(local_rows, dtype=jnp.int32)) & mine[..., None]
    ).astype(jnp.float32)
    arrival_hot = (arrival[..., None] == slot_range).astype(jnp.float32)
    placing = jnp.einsum("fcil,fcip->fclp", row_hot, arrival_hot, precision=highest)
    placed = jnp.einsum("fclp,fcpq->fclq", placing, incoming, precision=highest)
    column_range = jnp.arange(width, dtype=jnp.int32)

    def place_columns(inputs):
        rows_placed, indices = inputs
        column_hot = (indices[:, :, None] == column_range[None, None, :]).astype(jnp.float32)
        total = jnp.dot(
            rows_placed[0], column_hot[0], precision=highest, preferred_element_type=jnp.float32
        )
        return total + jnp.dot(
            rows_placed[1], column_hot[1], precision=highest, preferred_element_type=jnp.float32
        )

    added = lax.map(place_columns, (placed, child_map))
    pivot_local = front_pivot + added[:, :pivot_rows, :pivot_width]
    update_local = front_update + added[:, pivot_rows:, :]
    coupling = update_local[:, :, :pivot_width]
    trailing = update_local[:, :, pivot_width:]
    block = collect(pivot_local, "row", 1)
    inverse, pivots = factor(block)
    every_coupling = lax.all_gather(coupling, "row", axis=1, tiled=True)
    every_lhat = jnp.einsum("fik,fjk->fij", every_coupling, inverse, precision=highest)
    lhat = lax.dynamic_slice_in_dim(every_lhat, my_row * update_rows, update_rows, 1)
    scaled = lhat / pivots[:, None, :]
    correction = jnp.einsum("fik,fjk->fij", scaled, every_lhat, precision=highest)
    schur = trailing - correction
    negatives = jnp.sum(jnp.where(pivots < 0.0, 1.0, 0.0).astype(jnp.float32))
    total = taken_together(negatives, "col")
    negative_share = total / (fronts * lax.axis_size("col") * pivot_width)
    return (lhat, schur, negative_share)


def solution(mesh):
    in_specs = (
        P("col", "row", None),
        P("col", "row", None),
        P("col", None, "row", None),
        P("col", None, None),
    )
    out_specs = (P("col", "row", None), P("col", "row", None), P())
    return jax.shard_map(local, mesh=mesh, in_specs=in_specs, out_specs=out_specs, check_vma=False)
```

profile of v0, /device:TPU:0, one launch (start us, length us, event | category | flops | bytes accessed | tf_op | source)
XLA Modules:
  0.0 691.7 jit_solution(13084090968247595918)
XLA Ops:
  8.6 25.1 %fusion.17 = s32[16,2,16,32]{2,3,1,0:T(8,128)S(1)} fusion(s32[16,2,16,32]{2,3,1,0:T(8,128)S(1)} %copy.187), kind=kOutput, calls=%fused_computation.74 | output fusion | flops 9945088 | bytes 131072 | tf_op jit(solution)/shard_map/jit(cumsum)/reduce_window_sum | solution.py:93
  34.3 4.5 fusion.29
  38.8 5.2 reshape.308
  44.0 5.5 copy.192
  49.5 8.2 %all-to-all-start = ((f32[16,2,16,4,512]{4,3,1,0,2:T(4,128)}), f32[16,2,16,4,512]{4,3,1,0,2:T(4,128)}, u32[]{:S(2)}, u32[]{:S(2)}) async-start(f32[16,2,16,4,512]{4,3,1,0,2:T(4,128)} %copy.192), calls=%async_computation | async-start | bytes 8388608 | tf_op jit(solution)/shard_map/all_to_all | solution.py:106
  59.3 60.2 %all-to-all-done = f32[16,2,16,4,512]{4,3,1,0,2:T(4,128)} async-done(((f32[16,2,16,4,512]{4,3,1,0,2:T(4,128)}), f32[16,2,16,4,512]{4,3,1,0,2:T(4,128)}, u32[]{:S(2)}, u32[]{:S(2)}) %all-to-all-start) | async-done | bytes 4194336 | tf_op jit(solution)/shard_map/all_to_all | solution.py:106
  119.5 5.2 copy.193
  124.6 5.3 reshape.309
  130.0 6.8 fusion.58
  136.7 66.8 %while.33 = (s32[]{:T(128)}, f32[16,48,768]{2,1,0:T(8,128)}, f32[16,2,48,512]{3,2,1,0:T(8,128)}, s32[16,2,512]{2,1,0:T(2,128)S(1)}, s32[]{:T(128)}, /*index=5*/s32[]{:T(128)}, s32[]{}) while((s32[]{:T(128)}, f32[16,48,768]{2,1,0:T(8,128)}, f32[16,2,48,512]{3,2,1,0:T(8,128)}, s32[16,2,512]{2,1,0:T(2,128)S(1)}, s32[]{:T(128)}, ...), condition=%wide.region_3.4_spmd.clone, body=%wide.region_2.3_spmd.clone.sunk | while | flops 453808128 | bytes 2225761 | solution.py:127
  138.7 2.1 fusion.81
  142.9 2.2 fusion.81
  147.1 2.1 fusion.81
  151.2 2.2 fusion.81
  155.4 2.2 fusion.81
  159.6 2.2 fusion.81
  163.8 2.2 fusion.81
  167.9 2.2 fusion.81
  172.1 2.2 fusion.81
  176.3 2.2 fusion.81
  180.5 2.2 fusion.81
  184.6 2.1 fusion.81
  188.8 2.1 fusion.81
  193.0 2.1 fusion.81
  197.1 2.2 fusion.81
  201.3 2.2 fusion.81
  205.4 11.3 %all-to-all-start.1 = ((f32[16,16,8,128]{3,2,1,0:T(8,128)}), f32[16,16,8,128]{3,2,1,0:T(8,128)S(1)}, u32[]{:S(2)}, u32[]{:S(2)}) async-start(f32[16,16,8,128]{3,2,1,0:T(8,128)} %broadcast_in_dim.179), calls=%async_computation.1 | async-start | bytes 2097152 | tf_op jit(solution)/shard_map/all_to_all | solution.py:11
  217.1 2.4 slice_add_fusion
  220.3 12.2 %all-to-all-done.1 = f32[16,16,8,128]{3,2,1,0:T(8,128)S(1)} async-done(((f32[16,16,8,128]{3,2,1,0:T(8,128)}), f32[16,16,8,128]{3,2,1,0:T(8,128)S(1)}, u32[]{:S(2)}, u32[]{:S(2)}) %all-to-all-start.1) | async-done | bytes 1048608 | tf_op jit(solution)/shard_map/all_to_all | solution.py:11
  236.2 261.0 %while.34 = (s32[]{:T(128)}, f32[16,128,128]{1,2,0:T(8,128)S(1)}, f32[16,128,128]{1,2,0:T(8,128)}, f32[16,128]{0,1:T(8,128)S(1)}, s32[]{:T(128)}, /*index=5*/s32...) while((s32[]{:T(128)}, f32[16,128,128]{1,2,0:T(8,128)S(1)}, ...), condition=%wide.region_5.6_spmd.clone.clone, body=%wide.region_4.5_spmd.clone.clone.sunk | while | flops 26674340 | bytes 10079705 | solution.py:65
  236.2 7.5 %copy.242 = f32[16,128,128]{0,2,1:T(8,128)} copy(f32[16,128,128]{1,2,0:T(8,128)S(1)} %get-tuple-element.480) | data formatting | bytes 2097152 | tf_op jit(solution)/shard_map/while
  249.7 1.9 fusion.92
  252.6 7.5 %copy.242 = f32[16,128,128]{0,2,1:T(8,128)} copy(f32[16,128,128]{1,2,0:T(8,128)S(1)} %get-tuple-element.480) | data formatting | bytes 2097152 | tf_op jit(solution)/shard_map/while
  266.0 1.9 fusion.92
  268.9 7.5 %copy.242 = f32[16,128,128]{0,2,1:T(8,128)} copy(f32[16,128,128]{1,2,0:T(8,128)S(1)} %get-tuple-element.480) | data formatting | bytes 2097152 | tf_op jit(solution)/shard_map/while
  282.3 1.9 fusion.92
  285.2 7.5 %copy.242 = f32[16,128,128]{0,2,1:T(8,128)} copy(f32[16,128,128]{1,2,0:T(8,128)S(1)} %get-tuple-element.480) | data formatting | bytes 2097152 | tf_op jit(solution)/shard_map/while
  298.7 1.9 fusion.92
  301.5 7.5 %copy.242 = f32[16,128,128]{0,2,1:T(8,128)} copy(f32[16,128,128]{1,2,0:T(8,128)S(1)} %get-tuple-element.480) | data formatting | bytes 2097152 | tf_op jit(solution)/shard_map/while
  315.0 1.9 fusion.92
  317.8 7.5 %copy.242 = f32[16,128,128]{0,2,1:T(8,128)} copy(f32[16,128,128]{1,2,0:T(8,128)S(1)} %get-tuple-element.480) | data formatting | bytes 2097152 | tf_op jit(solution)/shard_map/while
  331.3 1.9 fusion.92
  334.1 7.5 %copy.242 = f32[16,128,128]{0,2,1:T(8,128)} copy(f32[16,128,128]{1,2,0:T(8,128)S(1)} %get-tuple-element.480) | data formatting | bytes 2097152 | tf_op jit(solution)/shard_map/while
  347.6 1.9 fusion.92
  350.4 7.5 %copy.242 = f32[16,128,128]{0,2,1:T(8,128)} copy(f32[16,128,128]{1,2,0:T(8,128)S(1)} %get-tuple-element.480) | data formatting | bytes 2097152 | tf_op jit(solution)/shard_map/while
  363.9 1.9 fusion.92
  366.8 7.5 %copy.242 = f32[16,128,128]{0,2,1:T(8,128)} copy(f32[16,128,128]{1,2,0:T(8,128)S(1)} %get-tuple-element.480) | data formatting | bytes 2097152 | tf_op jit(solution)/shard_map/while
  380.2 1.9 fusion.92
  383.1 7.5 %copy.242 = f32[16,128,128]{0,2,1:T(8,128)} copy(f32[16,128,128]{1,2,0:T(8,128)S(1)} %get-tuple-element.480) | data formatting | bytes 2097152 | tf_op jit(solution)/shard_map/while
  396.5 1.9 fusion.92
  399.4 7.5 %copy.242 = f32[16,128,128]{0,2,1:T(8,128)} copy(f32[16,128,128]{1,2,0:T(8,128)S(1)} %get-tuple-element.480) | data formatting | bytes 2097152 | tf_op jit(solution)/shard_map/while
  415.7 7.5 %copy.242 = f32[16,128,128]{0,2,1:T(8,128)} copy(f32[16,128,128]{1,2,0:T(8,128)S(1)} %get-tuple-element.480) | data formatting | bytes 2097152 | tf_op jit(solution)/shard_map/while
  429.1 1.9 fusion.92
  432.0 7.5 %copy.242 = f32[16,128,128]{0,2,1:T(8,128)} copy(f32[16,128,128]{1,2,0:T(8,128)S(1)} %get-tuple-element.480) | data formatting | bytes 2097152 | tf_op jit(solution)/shard_map/while
  448.3 7.5 %copy.242 = f32[16,128,128]{0,2,1:T(8,128)} copy(f32[16,128,128]{1,2,0:T(8,128)S(1)} %get-tuple-element.480) | data formatting | bytes 2097152 | tf_op jit(solution)/shard_map/while
  464.6 7.5 %copy.242 = f32[16,128,128]{0,2,1:T(8,128)} copy(f32[16,128,128]{1,2,0:T(8,128)S(1)} %get-tuple-element.480) | data formatting | bytes 2097152 | tf_op jit(solution)/shard_map/while
  478.1 1.9 fusion.92
  480.9 7.5 %copy.242 = f32[16,128,128]{0,2,1:T(8,128)} copy(f32[16,128,128]{1,2,0:T(8,128)S(1)} %get-tuple-element.480) | data formatting | bytes 2097152 | tf_op jit(solution)/shard_map/while
  494.4 1.9 fusion.92
  498.9 157.2 %custom-call.4 = f32[16,1,128,128]{2,3,1,0:T(8,128)S(1)} custom-call(f32[16,1,128,128]{3,2,1,0:T(8,128)S(1)} %add_bitcast_fusion), custom_call_target="InvertDiagBlocksLowerTriangular" | custom-call | tf_op jit(solution)/shard_map/vmap(jit(_solve_triangular))/triangular_solve | solution.py:68
  658.0 4.4 all-to-all-start.2
  664.2 3.4 all-to-all-done.2
  668.9 7.0 %fusion.59 = f32[16,640,128]{2,1,0:T(8,128)S(1)} fusion(f32[16,640,128]{2,1,0:T(8,128)} %all-gather.2.cloned.1.call-done, f32[16,128,128]{2,1,0:T(8,128)S(1)} %fusion.25), kind=kOutput, calls=%fused_computation.149 | convolution fusion | flops 2013265920 | bytes 11534336 | tf_op jit(solution)/shard_map/fik,fjk->fij/dot_general | solution.py:135
  676.0 7.7 %slice_subtract_fusion = f32[16,40,640]{2,1,0:T(8,128)} fusion(f32[16,40,768]{2,1,0:T(8,128)S(1)} %copy-done.3, f32[16,640,128]{2,1,0:T(8,128)S(1)} %fusion.59, f32[16,40,128]{2,1,0:T(8,128)S(1)} %constant_dynamic-slice_fusion.7, f32[16,128]{1,0:T(8,128)S(1)} %copy.199), kind=kOutput, calls=%fused_computation.83 | convolution fusion | flops 629637120 | bytes 8855552 | tf_op jit(solution)/shard_map/fik,fjk->fij/dot_general | solution.py:138
  (1095 shorter events, 160.4 us)
Async XLA Ops:
  7.2 27.2 %copy-start = (f32[16,2,32,512]{3,2,1,0:T(8,128)S(1)}, f32[16,2,32,512]{3,2,1,0:T(8,128)}, u32[]{:S(2)}) copy-start(f32[16,2,32,512]{3,2,1,0:T(8,128)} %param.10) | copy-start | bytes 6291460
  49.5 8.3 %copy-start.5 = (s32[16,2,512]{2,1,0:T(2,128)S(1)}, s32[16,2,512]{2,1,0:T(2,128)}, u32[]{:S(2)}) copy-start(s32[16,2,512]{2,1,0:T(2,128)} %param.11) | copy-start | bytes 196612
  49.5 69.9 %all-to-all-start = ((f32[16,2,16,4,512]{4,3,1,0,2:T(4,128)}), f32[16,2,16,4,512]{4,3,1,0,2:T(4,128)}, u32[]{:S(2)}, u32[]{:S(2)}) async-start(f32[16,2,16,4,512]{4,3,1,0,2:T(4,128)} %copy.192), calls=%async_computation | async-start | bytes 8388608 | tf_op jit(solution)/shard_map/all_to_all | solution.py:106
  136.7 66.8 %copy-start.6 = (f32[16,8,128]{2,1,0:T(8,128)S(1)}, f32[16,8,128]{2,1,0:T(8,128)}, u32[]{:S(2)}) copy-start(f32[16,8,128]{2,1,0:T(8,128)} %param.8) | copy-start | bytes 196612
  205.4 27.1 %all-to-all-start.1 = ((f32[16,16,8,128]{3,2,1,0:T(8,128)}), f32[16,16,8,128]{3,2,1,0:T(8,128)S(1)}, u32[]{:S(2)}, u32[]{:S(2)}) async-start(f32[16,16,8,128]{3,2,1,0:T(8,128)} %broadcast_in_dim.179), calls=%async_computation.1 | async-start | bytes 2097152 | tf_op jit(solution)/shard_map/all_to_all | solution.py:11
  216.7 452.2 %all-gather.2.cloned.1.call-start = ((), (), s32[]{:S(2)}) async-start(), calls=%async_computation.3 | async-start | bytes 5570560 | tf_op jit(solution)/shard_map/all_gather | solution.py:134
  219.5 14.1 %copy-start.2 = (f32[16,40,768]{2,1,0:T(8,128)}, f32[16,40,768]{2,1,0:T(8,128)S(1)}, u32[]{:S(2)}) copy-start(f32[16,40,768]{2,1,0:T(8,128)S(1)} %slice_add_fusion) | copy-start | bytes 5898244
  658.0 9.7 %all-to-all-start.2 = ((f32[8,1,1]{2,1,0:T(1,128)}), f32[8,1,1]{2,1,0:T(1,128)S(1)}, u32[]{:S(2)}, u32[]{:S(2)}) async-start(f32[8,1,1]{2,1,0:T(1,128)} %broadcast_in_dim.182), calls=%async_computation.2 | async-start | bytes 8192 | tf_op jit(solution)/shard_map/all_to_all | solution.py:11
  668.9 7.1 %copy-start.3 = (f32[16,40,768]{2,1,0:T(8,128)S(1)}, f32[16,40,768]{2,1,0:T(8,128)}, u32[]{:S(2)}) copy-start(f32[16,40,768]{2,1,0:T(8,128)} %copy-done.2) | copy-start | bytes 5898244
  675.9 7.8 %copy-start.1 = (f32[16,2,32,512]{3,2,1,0:T(8,128)S(1)}, f32[16,2,32,512]{3,2,1,0:T(8,128)}, u32[]{:S(2)}) copy-start(f32[16,2,32,512]{3,2,1,0:T(8,128)} %param.10) | copy-start | bytes 6291460
  676.0 7.7 %copy-start.4 = (f32[16,40,128]{2,1,0:T(8,128)}, f32[16,40,128]{2,1,0:T(8,128)S(1)}, u32[]{:S(2)}) copy-start(f32[16,40,128]{2,1,0:T(8,128)S(1)} %constant_dynamic-slice_fusion.7) | copy-start | bytes 983044
Sparse Core Ops, SparseCore 0:
  220.4 58.0 all-gather.1
where the time goes:
time: 695 us; the launch traced here: 692 us
  local copies, waits for them, and re-layouts  227 us (33%)
  other arithmetic  227 us (33%)
  matrix products  117 us (17%)
  waiting for transfers between devices  75.9 us (11%)
  starting transfers between devices  24.2 us (3%)
  between operations  16.1 us (2%)
    another operation x4, other arithmetic, factor(): jax.scipy.linalg.solve_triangular(matrix, identity, lower=True, unit_diag...  157 us
    while x48, local copies, waits for them, and re-layouts  131 us
    all_to_all x1, waiting for transfers between devices, local(): lax.all_to_all(outgoing, 'row', split_axis=2, concat_axis=2, tiled=True)  60.2 us
    dot_general x16, matrix products, place_columns(): jnp.dot(rows_placed[0], column_hot[0], precision=highest, preferred_eleme...  34.5 us
    dot_general x16, matrix products, panel_step(): jnp.einsum('fiw,fjw->fij', panel_lower * panel_pivots[:, None, :], panel_...  30 us
    squeeze x128, local copies, waits for them, and re-layouts, panel_step(): leading = lax.dynamic_index_in_dim(strip, place, 1, keepdims=False)  27.7 us
    another operation x1, other arithmetic, local(): earlier = jnp.cumsum(blocked, axis=3) - blocked  25.1 us
    dot_general x16, matrix products, place_columns(): jnp.dot(rows_placed[1], column_hot[1], precision=highest, preferred_eleme...  23.9 us
  transfers between devices with their start and end apart: 4, of which 3 were waited for; matrix products, arithmetic and copies ran while one was open for 62% of the time, Pallas kernels for 0%

commit v1 on v0

v1 whole, which is shorter than its diff:
```python
import functools

import jax
import jax.numpy as jnp
from jax import lax
from jax.experimental import pallas as pl
from jax.experimental.pallas import tpu as pltpu
from jax.sharding import PartitionSpec as P

MESH = pl.DeviceIdType.MESH
F32 = jnp.float32
BF16 = jnp.bfloat16
HIGHEST = lax.Precision.HIGHEST

N_ROW = 16
N_COL = 8
SIDE = 4
S = 128
CU = 512
U = 640
F = 768
SP = 8
UP = 40
HELD = 32
OFFSETS = [(dx, dz) for dx in range(SIDE) for dz in range(SIDE) if (dx, dz) != (0, 0)]


def peer(me, dx, dz):
    x = lax.rem(me // SIDE + dx, SIDE)
    z = lax.rem(lax.rem(me, SIDE) + dz, SIDE)
    return x * SIDE + z


def greet(row_peers, col_peers):
    barrier = pltpu.get_barrier_semaphore()
    for other in row_peers:
        pl.semaphore_signal(barrier, inc=1, device_id={"row": other}, device_id_type=MESH)
    for other in col_peers:
        pl.semaphore_signal(barrier, inc=1, device_id={"col": other}, device_id_type=MESH)
    pl.semaphore_wait(barrier, len(row_peers) + len(col_peers))


def gather_kernel(
    child_ref, pivot_ref, update_ref, near_ref, next_ref, far_ref, panel_ref, send_sem, recv_sem, own_sem
):
    me = lax.axis_index("row")
    group = me // SIDE
    near = pl.multiple_of(group * 128, 128)
    following = pl.multiple_of(lax.rem(group + 1, 4) * 128, 128)
    opposite = pl.multiple_of(lax.rem(group + 2, 4) * 128, 128)
    far_child = group // 2
    rows = pl.ds(pl.multiple_of(me * HELD, HELD), HELD)
    pivot_rows = pl.ds(pl.multiple_of(me * SP, SP), SP)
    update_rows = pl.ds(pl.multiple_of(S + me * UP, SP), UP)

    def pieces(front):
        return (
            (pivot_ref.at[front], panel_ref.at[pivot_rows]),
            (child_ref.at[front, :, :, pl.ds(near, 128)], near_ref.at[:, rows]),
            (child_ref.at[front, :, :, pl.ds(following, 128)], next_ref.at[:, rows]),
            (child_ref.at[front, far_child, :, pl.ds(opposite, 128)], far_ref.at[rows]),
            (update_ref.at[front, :, pl.ds(0, S)], panel_ref.at[update_rows]),
        )

    own = [
        pltpu.make_async_copy(source, target, own_sem.at[i])
        for i, (source, target) in enumerate(pieces(me))
    ]
    for copy in own:
        copy.start()
    others = [peer(me, dx, dz) for dx, dz in OFFSETS]
    greet(others, [])
    copies = []
    for place, other in enumerate(others):
        for i, (source, target) in enumerate(pieces(other)):
            copies.append(
                pltpu.make_async_remote_copy(
                    src_ref=source,
                    dst_ref=target,
                    send_sem=send_sem.at[place, i],
                    recv_sem=recv_sem.at[place, i],
                    device_id={"row": other},
                    device_id_type=MESH,
                )
            )
            copies[-1].start()
    for copy in own:
        copy.wait()
    for copy in copies:
        copy.wait()


def gather(child_blocks, front_pivot, front_update):
    any_spec = pl.BlockSpec(memory_space=pl.ANY)
    vmem_spec = pl.BlockSpec(memory_space=pltpu.VMEM)
    return pl.pallas_call(
        gather_kernel,
        out_shape=(
            jax.ShapeDtypeStruct((2, CU, 128), F32),
            jax.ShapeDtypeStruct((2, CU, 128), F32),
            jax.ShapeDtypeStruct((CU, 128), F32),
            jax.ShapeDtypeStruct((F, S), F32),
        ),
        in_specs=[any_spec] * 3,
        out_specs=(vmem_spec,) * 4,
        scratch_shapes=[
            pltpu.SemaphoreType.DMA((len(OFFSETS), 5)),
            pltpu.SemaphoreType.DMA((len(OFFSETS), 5)),
            pltpu.SemaphoreType.DMA((5,)),
        ],
        compiler_params=pltpu.CompilerParams(collective_id=0, has_side_effects=True),
        name="gather_fronts",
    )(child_blocks, front_pivot, front_update)


def split(values):
    high = values.astype(BF16)
    low = (values - high.astype(F32)).astype(BF16)
    return high, low


def nt_dot(a, b, precision=None):
    return lax.dot_general(
        a, b, (((1,), (1,)), ((), ())), precision=precision, preferred_element_type=F32
    )


BLOCK = 32


def factor_in_place(work):
    sub = lax.broadcasted_iota(jnp.int32, (8, 128), 0)
    groups = BLOCK // 8
    for block in range(S // BLOCK):
        base = block * BLOCK
        left = [work[base + 8 * g : base + 8 * g + 8, 0:128] for g in range(groups)]
        right = [work[base + 8 * g : base + 8 * g + 8, 128:256] for g in range(groups)]
        for step in range(BLOCK):
            k = base + step
            own, inner = step // 8, step % 8
            row_left = jnp.broadcast_to(left[own][inner : inner + 1, :], (8, 128))
            row_right = jnp.broadcast_to(right[own][inner : inner + 1, :], (8, 128))
            pivot = jnp.broadcast_to(row_left[:, k : k + 1], (8, 128))
            scale = 1.0 / pivot
            for g in range(own, groups):
                column = jnp.broadcast_to(left[g][:, k : k + 1], (8, 128))
                multiplier = column * scale
                if g == own:
                    multiplier = jnp.where(sub > inner, multiplier, 0.0)
                left[g] = left[g] - multiplier * row_left
                right[g] = right[g] - multiplier * row_right
        strip_left = jnp.concatenate(left, axis=0)
        strip_right = jnp.concatenate(right, axis=0)
        work[base : base + BLOCK, 0:128] = strip_left
        work[base : base + BLOCK, 128:256] = strip_right
        after = base + BLOCK
        if after < S:
            lanes = lax.broadcasted_iota(jnp.int32, (BLOCK, 128), 1)
            places = lax.broadcasted_iota(jnp.int32, (BLOCK, 128), 0) + base
            diagonal = jnp.sum(
                jnp.where(lanes == places, strip_left, 0.0), axis=1, keepdims=True
            )
            lower = strip_left / diagonal
            strip = jnp.concatenate([strip_left, strip_right], axis=1)
            product = lax.dot_general(
                lower, strip, (((0,), (0,)), ((), ())), precision=HIGHEST, preferred_element_type=F32
            )
            work[after:S, :] = work[after:S, :] - product[after:S, :]


def front_kernel(
    map_ref, near_ref, next_ref, far_ref, panel_ref, lhat_ref, rest_ref, negative_ref, hot_ref, work, high_ref, low_ref
):
    me = lax.axis_index("row")
    for child in range(2):
        indices = map_ref[me, child : child + 1, :]
        position = lax.broadcasted_iota(jnp.int32, (F, CU), 0)
        hot_ref[child] = jnp.where(indices == position, 1.0, 0.0).astype(BF16)

    def fill(child, i, j, block):
        high, low = split(block)
        high_ref[child, 128 * i : 128 * i + 128, 128 * j : 128 * j + 128] = high
        low_ref[child, 128 * i : 128 * i + 128, 128 * j : 128 * j + 128] = low

    for child in range(2):
        for i in range(4):
            rows = slice(128 * i, 128 * i + 128)
            fill(child, i, i, near_ref[child, rows, :])
            block = next_ref[child, rows, :]
            fill(child, i, (i + 1) % 4, block)
            fill(child, (i + 1) % 4, i, block.T)
    for i in range(4):
        child = i // 2
        block = far_ref[128 * i : 128 * i + 128, :]
        fill(child, i, (i + 2) % 4, block)
        fill(child, (i + 2) % 4, i, block.T)

    spread = []
    for child in range(2):
        hot = hot_ref[child]
        high = jnp.dot(hot, high_ref[child], preferred_element_type=F32).astype(BF16)
        low = jnp.dot(hot, low_ref[child], preferred_element_type=F32).astype(BF16)
        spread.append((high, low))

    def columns(start, size, first=0):
        total = None
        for child in range(2):
            hot = hot_ref[child, start : start + size, :]
            for part in spread[child]:
                term = nt_dot(part[first:, :], hot)
                total = term if total is None else total + term
        return total

    panel = panel_ref[...] + columns(0, S)
    lane = lax.broadcasted_iota(jnp.int32, (S, S), 1)
    place = lax.broadcasted_iota(jnp.int32, (S, S), 0)
    work[:, 0:128] = panel[:S]
    work[:, 128:256] = jnp.where(lane == place, 1.0, 0.0)
    factor_in_place(work)
    inverse = work[:, 128:256]
    pivots = jnp.sum(jnp.where(lane == place, work[:, 0:128], 0.0), axis=0, keepdims=True)
    negative_ref[0] = jnp.where(pivots < 0.0, 1.0, 0.0)
    lhat = nt_dot(panel[S:], inverse, HIGHEST)
    lhat_ref[...] = lhat
    scaled = lhat / pivots
    for start in range(0, U, 128):
        correction = nt_dot(scaled, lhat[start : start + 128], HIGHEST)
        rest_ref[:, start : start + 128] = columns(S + start, 128, S) - correction


def front(child_map, near, following, far, panel):
    vmem_spec = pl.BlockSpec(memory_space=pltpu.VMEM)
    return pl.pallas_call(
        front_kernel,
        out_shape=(
            jax.ShapeDtypeStruct((U, S), F32),
            jax.ShapeDtypeStruct((U, U), F32),
            jax.ShapeDtypeStruct((1, 1, S), F32),
        ),
        in_specs=[vmem_spec] * 5,
        out_specs=(vmem_spec,) * 3,
        scratch_shapes=[
            pltpu.VMEM((2, F, CU), BF16),
            pltpu.VMEM((S, 2 * S), F32),
            pltpu.VMEM((2, CU, CU), BF16),
            pltpu.VMEM((2, CU, CU), BF16),
        ],
        name="front_factor",
    )(child_map, near, following, far, panel)


def scatter_kernel(
    lhat_ref, rest_ref, negative_ref, lhat_out, rest_out, share_out,
    counts, send_sem, recv_sem, count_send, count_recv, row_send, row_recv, own_sem
):
    me = lax.axis_index("row")
    col = lax.axis_index("col")
    others = [peer(me, dx, dz) for dx, dz in OFFSETS]
    columns = [lax.rem(col + d, N_COL) for d in range(1, N_COL)]

    def rows(row):
        return pl.ds(pl.multiple_of(row * UP, SP), UP)

    own = [
        pltpu.make_async_copy(negative_ref, counts.at[me, pl.ds(col, 1)], own_sem.at[0]),
        pltpu.make_async_copy(lhat_ref.at[rows(me)], lhat_out.at[me], own_sem.at[1]),
        pltpu.make_async_copy(rest_ref.at[rows(me)], rest_out.at[me], own_sem.at[2]),
    ]
    for copy in own:
        copy.start()
    greet(others, columns)
    tallies = []
    for place, other in enumerate(columns):
        tallies.append(
            pltpu.make_async_remote_copy(
                src_ref=negative_ref,
                dst_ref=counts.at[me, pl.ds(col, 1)],
                send_sem=count_send.at[place],
                recv_sem=count_recv.at[place],
                device_id={"col": other},
                device_id_type=MESH,
            )
        )
        tallies[-1].start()
    copies = []
    for place, other in enumerate(others):
        for i, (source, target) in enumerate(((lhat_ref, lhat_out), (rest_ref, rest_out))):
            copies.append(
                pltpu.make_async_remote_copy(
                    src_ref=source.at[rows(other)],
                    dst_ref=target.at[me],
                    send_sem=send_sem.at[place, i],
                    recv_sem=recv_sem.at[place, i],
                    device_id={"row": other},
                    device_id_type=MESH,
                )
            )
            copies[-1].start()
    for copy in own:
        copy.wait()
    for copy in tallies:
        copy.wait()
    forwards = []
    for place, other in enumerate(others):
        forwards.append(
            pltpu.make_async_remote_copy(
                src_ref=counts.at[me],
                dst_ref=counts.at[me],
                send_sem=row_send.at[place],
                recv_sem=row_recv.at[place],
                device_id={"row": other},
                device_id_type=MESH,
            )
        )
        forwards[-1].start()
    for copy in copies:
        copy.wait()
    for copy in forwards:
        copy.wait()
    total = counts[0]
    for row in range(1, N_ROW):
        total = total + counts[row]
    flat = jnp.sum(total, axis=0)
    share_out[...] = jnp.sum(flat, axis=1, keepdims=True) / float(N_ROW * N_COL * S)


def scatter(lhat, rest, negative):
    any_spec = pl.BlockSpec(memory_space=pl.ANY)
    vmem_spec = pl.BlockSpec(memory_space=pltpu.VMEM)
    count = len(OFFSETS)
    return pl.pallas_call(
        scatter_kernel,
        out_shape=(
            jax.ShapeDtypeStruct((N_ROW, UP, S), F32),
            jax.ShapeDtypeStruct((N_ROW, UP, U), F32),
            jax.ShapeDtypeStruct((1, 1), F32),
        ),
        in_specs=[any_spec] * 3,
        out_specs=(vmem_spec,) * 3,
        scratch_shapes=[
            pltpu.VMEM((N_ROW, N_COL, 1, S), F32),
            pltpu.SemaphoreType.DMA((count, 2)),
            pltpu.SemaphoreType.DMA((count, 2)),
            pltpu.SemaphoreType.DMA((N_COL - 1,)),
            pltpu.SemaphoreType.DMA((N_COL - 1,)),
            pltpu.SemaphoreType.DMA((count,)),
            pltpu.SemaphoreType.DMA((count,)),
            pltpu.SemaphoreType.DMA((3,)),
        ],
        compiler_params=pltpu.CompilerParams(collective_id=1, has_side_effects=True),
        name="scatter_fronts",
    )(lhat, rest, negative)


def local(front_pivot, front_update, child_blocks, child_map):
    near, following, far, panel = gather(child_blocks, front_pivot, front_update)
    lhat, rest, negative = front(child_map, near, following, far, panel)
    lhat, rest, share = scatter(lhat, rest, negative)
    return (lhat, front_update[:, :, S:] + rest, share[0, 0])


def solution(mesh):
    in_specs = (
        P("col", "row", None),
        P("col", "row", None),
        P("col", None, "row", None),
        P("col", None, None),
    )
    out_specs = (P("col", "row", None), P("col", "row", None), P())
    return jax.shard_map(local, mesh=mesh, in_specs=in_specs, out_specs=out_specs, check_vma=False)
```

time: 695 us -> 105 us (0.15)
  local copies, waits for them, and re-layouts: 227 us -> 0.73 us
  other arithmetic: 227 us -> 2.8 us
  matrix products: 117 us -> 0 us
  Pallas kernels: 0 us -> 99.2 us
  waiting for transfers between devices: 75.9 us -> 0 us
  starting transfers between devices: 24.2 us -> 0 us
  between operations: 16.1 us -> 2.35 us
    another operation x5 -> x0, other arithmetic: 182 us -> none  [the longest x4 157 us: factor(): jax.scipy.linalg.solve_triangular(matrix, identity, lower=True, unit_diag...]
    while x50 -> x0, local copies, waits for them, and re-layouts: 132 us -> none
    dot_general x53 -> x0, matrix products: 116 us -> none  [the longest x16 34.5 us: place_columns(): jnp.dot(rows_placed[0], column_hot[0], precision=highest, preferred_eleme...]
    pallas_call x0 -> x3, Pallas kernels: none -> 99.2 us  [the longest x1 36.9 us: scatter(): pl.pallas_call(scatter_kernel, out_shape=(jax.ShapeDtypeStruct((N_ROW, UP...]
    all_to_all x3 -> x0, waiting for transfers between devices: 75.8 us -> none  [the longest x1 60.2 us: local(): lax.all_to_all(outgoing, 'row', split_axis=2, concat_axis=2, tiled=True)]
    squeeze x128 -> x0, local copies, waits for them, and re-layouts: 27.7 us -> none  [panel_step(): leading = lax.dynamic_index_in_dim(strip, place, 1, keepdims=False)]
    all_to_all x3 -> x0, starting transfers between devices: 23.9 us -> none  [the longest x2 15.7 us: from_everyone(): return lax.all_to_all(copies, axis, split_axis=0, concat_axis=0, tiled=True)]
    dynamic_slice x228 -> x0, local copies, waits for them, and re-layouts: 23.6 us -> none  [the longest x224 23.5 us: panel_step(): leading = lax.dynamic_index_in_dim(strip, place, 1, keepdims=False)]
  transfers between devices with their start and end apart: 4 -> 0, of which waited for: 3 -> 0; matrix products, arithmetic and copies ran while one was open for 62% -> 0% of each run, Pallas kernels for 0% -> 0%
where the time goes in v1:
time: 105 us
  Pallas kernels  99.2 us (94%)
  other arithmetic  2.8 us (3%)
  between operations  2.35 us (2%)
    pallas_call x1, Pallas kernels, scatter(): pl.pallas_call(scatter_kernel, out_shape=(jax.ShapeDtypeStruct((N_ROW, UP...  36.9 us
    pallas_call x1, Pallas kernels, gather(): pl.pallas_call(gather_kernel, out_shape=(jax.ShapeDtypeStruct((2, CU, 128...  33.9 us
    pallas_call x1, Pallas kernels, front(): pl.pallas_call(front_kernel, out_shape=(jax.ShapeDtypeStruct((U, S), F32)...  28.5 us
    add x1, other arithmetic, local(): return (lhat, front_update[:, :, S:] + rest, share[0, 0])  2.8 us

profile of v1, /device:TPU:0, one launch (start us, length us, event | category | flops | bytes accessed | tf_op | source)
XLA Modules:
  0.0 105.1 jit_solution(6484307748940489458)
XLA Ops:
  0.6 33.9 %gather_fronts.1 = (f32[2,512,128]{2,1,0:T(8,128)}, f32[2,512,128]{2,1,0:T(8,128)}, f32[512,128]{1,0:T(8,128)}, f32[768,128]{1,0:T(8,128)}) custom-call(f32[16,2,32,512]{3,2,1,0:T(8,128)} %child_ref.1, f32[16,8,128]{2,1,0:T(8,128)} %pivot_ref.1, f32[16,40,768]{2,1,0:T(8,128)} %update_ref.1), custom_call_target="tpu_custom_call" | custom-call | tf_op jit(solution)/shard_map/gather_fronts/pallas_call | solution.py:96
  34.5 0.0 copy-start
  34.5 28.5 %front_factor.1 = (f32[640,128]{1,0:T(8,128)}, f32[640,640]{1,0:T(8,128)}, f32[1,1,128]{2,1,0:T(1,128)}) custom-call(s32[16,2,512]{2,1,0:T(2,128)} %map_ref.1, f32[2,512,128]{2,1,0:T(8,128)} %get-tuple-element.13.near_ref, f32[2,512,128]{2,1,0:T(8,128)} %get-tuple-element.14.next_ref, f32[512,128]{1,0:T(8,128)} %get-tuple-element.15.far_ref, ...), custom_call_target="tpu_custom_call" | custom-call | tf_op jit(solution)/shard_map/front_factor/pallas_call | solution.py:233
  63.0 36.9 %scatter_fronts.1 = (f32[16,40,128]{2,1,0:T(8,128)}, f32[16,40,640]{2,1,0:T(8,128)}, f32[1,1]{1,0:T(1,128)}) custom-call(f32[640,128]{1,0:T(8,128)} %get-tuple-element.17.lhat_ref, f32[640,640]{1,0:T(8,128)} %get-tuple-element.18.rest_ref, f32[1,1,128]{2,1,0:T(1,128)} %get-tuple-element.19.negative_ref), custom_call_target="tpu_custom_call" | custom-call | tf_op jit(solution)/shard_map/scatter_fronts/pallas_call | solution.py:331
  99.9 0.0 copy-done
  99.9 0.0 copy-start.1
  99.9 2.8 %slice_add_fusion = f32[16,40,640]{2,1,0:T(8,128)} fusion(f32[16,40,640]{2,1,0:T(8,128)} %get-tuple-element.21, f32[16,40,768]{2,1,0:T(8,128)S(1)} %copy-done), kind=kLoop, calls=%fused_computation | loop fusion | flops 409600 | bytes 4915200 | tf_op jit(solution)/shard_map/add | solution.py:359
  102.7 0.0 copy-done.1
  102.7 0.7 copy.9
Async XLA Ops:
  34.5 65.4 %copy-start = (f32[16,40,768]{2,1,0:T(8,128)S(1)}, f32[16,40,768]{2,1,0:T(8,128)}, u32[]{:S(2)}) copy-start(f32[16,40,768]{2,1,0:T(8,128)} %update_ref.1) | copy-start | bytes 5898244
  99.9 2.8 %copy-start.1 = (f32[16,40,128]{2,1,0:T(8,128)S(1)}, f32[16,40,128]{2,1,0:T(8,128)}, u32[]{:S(2)}) copy-start(f32[16,40,128]{2,1,0:T(8,128)} %get-tuple-element.26) | copy-start | bytes 983044

commit v2 on v1

--- a/solution.py
+++ b/solution.py
@@ -22,7 +22,12 @@
 SP = 8
 UP = 40
 HELD = 32
-OFFSETS = [(dx, dz) for dx in range(SIDE) for dz in range(SIDE) if (dx, dz) != (0, 0)]
+OFFSETS = [
+    (dx, (dx + turn) % SIDE)
+    for turn in range(SIDE)
+    for dx in range(SIDE)
+    if (dx, (dx + turn) % SIDE) != (0, 0)
+]
 
 
 def peer(me, dx, dz):

time: 105 us -> 99.9 us (0.951); the launches traced: 105 us -> 98.9 us
  Pallas kernels: 99.2 us -> 93 us
    pallas_call x1, Pallas kernels: 36.9 us -> 33.1 us  [scatter(): pl.pallas_call(scatter_kernel, out_shape=(jax.ShapeDtypeStruct((N_ROW, UP...]
    pallas_call x1, Pallas kernels: 33.9 us -> 31.4 us  [gather(): pl.pallas_call(gather_kernel, out_shape=(jax.ShapeDtypeStruct((2, CU, 128...]
where the time goes in v2:
time: 99.9 us; the launch traced here: 98.9 us
  Pallas kernels  93 us (93%)
  other arithmetic  2.8 us (3%)
  between operations  2.35 us (2%)
    pallas_call x1, Pallas kernels, scatter(): pl.pallas_call(scatter_kernel, out_shape=(jax.ShapeDtypeStruct((N_ROW, UP...  33.1 us
    pallas_call x1, Pallas kernels, gather(): pl.pallas_call(gather_kernel, out_shape=(jax.ShapeDtypeStruct((2, CU, 128...  31.4 us
    pallas_call x1, Pallas kernels, front(): pl.pallas_call(front_kernel, out_shape=(jax.ShapeDtypeStruct((U, S), F32)...  28.5 us
    add x1, other arithmetic, local(): return (lhat, front_update[:, :, S:] + rest, share[0, 0])  2.8 us

profile of v2, /device:TPU:0, one launch (start us, length us, event | category | flops | bytes accessed | tf_op | source)
XLA Modules:
  0.0 98.9 jit_solution(406222470989978661)
XLA Ops:
  0.6 31.4 %gather_fronts.1 = (f32[2,512,128]{2,1,0:T(8,128)}, f32[2,512,128]{2,1,0:T(8,128)}, f32[512,128]{1,0:T(8,128)}, f32[768,128]{1,0:T(8,128)}) custom-call(f32[16,2,32,512]{3,2,1,0:T(8,128)} %child_ref.1, f32[16,8,128]{2,1,0:T(8,128)} %pivot_ref.1, f32[16,40,768]{2,1,0:T(8,128)} %update_ref.1), custom_call_target="tpu_custom_call" | custom-call | tf_op jit(solution)/shard_map/gather_fronts/pallas_call | solution.py:101
  32.0 0.0 copy-start
  32.0 28.5 %front_factor.1 = (f32[640,128]{1,0:T(8,128)}, f32[640,640]{1,0:T(8,128)}, f32[1,1,128]{2,1,0:T(1,128)}) custom-call(s32[16,2,512]{2,1,0:T(2,128)} %map_ref.1, f32[2,512,128]{2,1,0:T(8,128)} %get-tuple-element.13.near_ref, f32[2,512,128]{2,1,0:T(8,128)} %get-tuple-element.14.next_ref, f32[512,128]{1,0:T(8,128)} %get-tuple-element.15.far_ref, ...), custom_call_target="tpu_custom_call" | custom-call | tf_op jit(solution)/shard_map/front_factor/pallas_call | solution.py:238
  60.5 33.1 %scatter_fronts.1 = (f32[16,40,128]{2,1,0:T(8,128)}, f32[16,40,640]{2,1,0:T(8,128)}, f32[1,1]{1,0:T(1,128)}) custom-call(f32[640,128]{1,0:T(8,128)} %get-tuple-element.17.lhat_ref, f32[640,640]{1,0:T(8,128)} %get-tuple-element.18.rest_ref, f32[1,1,128]{2,1,0:T(1,128)} %get-tuple-element.19.negative_ref), custom_call_target="tpu_custom_call" | custom-call | tf_op jit(solution)/shard_map/scatter_fronts/pallas_call | solution.py:336
  93.6 0.0 copy-done
  93.7 0.0 copy-start.1
  93.7 2.8 %slice_add_fusion = f32[16,40,640]{2,1,0:T(8,128)} fusion(f32[16,40,640]{2,1,0:T(8,128)} %get-tuple-element.21, f32[16,40,768]{2,1,0:T(8,128)S(1)} %copy-done), kind=kLoop, calls=%fused_computation | loop fusion | flops 409600 | bytes 4915200 | tf_op jit(solution)/shard_map/add | solution.py:364
  96.5 0.0 copy-done.1
  96.5 0.7 copy.9
Async XLA Ops:
  32.0 61.6 %copy-start = (f32[16,40,768]{2,1,0:T(8,128)S(1)}, f32[16,40,768]{2,1,0:T(8,128)}, u32[]{:S(2)}) copy-start(f32[16,40,768]{2,1,0:T(8,128)} %update_ref.1) | copy-start | bytes 5898244
  93.7 2.8 %copy-start.1 = (f32[16,40,128]{2,1,0:T(8,128)S(1)}, f32[16,40,128]{2,1,0:T(8,128)}, u32[]{:S(2)}) copy-start(f32[16,40,128]{2,1,0:T(8,128)} %get-tuple-element.26) | copy-start | bytes 983044

commit v3 on v2

--- a/solution.py
+++ b/solution.py
@@ -133,6 +133,14 @@
 BLOCK = 32
 
 
+def spread_lane(values, lane):
+    return jnp.broadcast_to(values[:, lane : lane + 1], (8, 128))
+
+
+def spread_row(values, row):
+    return jnp.broadcast_to(values[row : row + 1, :], (8, 128))
+
+
 def factor_in_place(work):
     sub = lax.broadcasted_iota(jnp.int32, (8, 128), 0)
     groups = BLOCK // 8
@@ -140,20 +148,24 @@
         base = block * BLOCK
         left = [work[base + 8 * g : base + 8 * g + 8, 0:128] for g in range(groups)]
         right = [work[base + 8 * g : base + 8 * g + 8, 128:256] for g in range(groups)]
-        for step in range(BLOCK):
-            k = base + step
-            own, inner = step // 8, step % 8
-            row_left = jnp.broadcast_to(left[own][inner : inner + 1, :], (8, 128))
-            row_right = jnp.broadcast_to(right[own][inner : inner + 1, :], (8, 128))
-            pivot = jnp.broadcast_to(row_left[:, k : k + 1], (8, 128))
-            scale = 1.0 / pivot
-            for g in range(own, groups):
-                column = jnp.broadcast_to(left[g][:, k : k + 1], (8, 128))
-                multiplier = column * scale
-                if g == own:
-                    multiplier = jnp.where(sub > inner, multiplier, 0.0)
-                left[g] = left[g] - multiplier * row_left
-                right[g] = right[g] - multiplier * row_right
+        for panel in range(groups):
+            active = range(panel, groups)
+            columns = [
+                {g: spread_lane(left[g], base + 8 * panel + j) for g in active} for j in range(8)
+            ]
+            for j in range(8):
+                scale = 1.0 / spread_row(columns[j][panel], j)
+                row_left = spread_row(left[panel], j)
+                row_right = spread_row(right[panel], j)
+                across = {i: spread_row(columns[i][panel], j) for i in range(j + 1, 8)}
+                for g in active:
+                    multiplier = columns[j][g] * scale
+                    if g == panel:
+                        multiplier = jnp.where(sub > j, multiplier, 0.0)
+                    for i in range(j + 1, 8):
+                        columns[i][g] = columns[i][g] - multiplier * across[i]
+                    left[g] = left[g] - multiplier * row_left
+                    right[g] = right[g] - multiplier * row_right
         strip_left = jnp.concatenate(left, axis=0)
         strip_right = jnp.concatenate(right, axis=0)
         work[base : base + BLOCK, 0:128] = strip_left

time: 99.9 us -> 87.6 us (0.88)
  Pallas kernels: 93 us -> 80.6 us
    pallas_call x1, Pallas kernels: 28.5 us -> 16.1 us  [front(): pl.pallas_call(front_kernel, out_shape=(jax.ShapeDtypeStruct((U, S), F32)...]
where the time goes in v3:
time: 87.6 us; the launch traced here: 86.5 us
  Pallas kernels  80.6 us (92%)
  other arithmetic  2.8 us (3%)
  between operations  2.35 us (3%)
    pallas_call x1, Pallas kernels, scatter(): pl.pallas_call(scatter_kernel, out_shape=(jax.ShapeDtypeStruct((N_ROW, UP...  33.1 us
    pallas_call x1, Pallas kernels, gather(): pl.pallas_call(gather_kernel, out_shape=(jax.ShapeDtypeStruct((2, CU, 128...  31.4 us
    pallas_call x1, Pallas kernels, front(): pl.pallas_call(front_kernel, out_shape=(jax.ShapeDtypeStruct((U, S), F32)...  16.1 us
    add x1, other arithmetic, local(): return (lhat, front_update[:, :, S:] + rest, share[0, 0])  2.8 us

profile of v3, /device:TPU:0, one launch (start us, length us, event | category | flops | bytes accessed | tf_op | source)
XLA Modules:
  0.0 86.5 jit_solution(102561264863513497)
XLA Ops:
  0.6 31.4 %gather_fronts.1 = (f32[2,512,128]{2,1,0:T(8,128)}, f32[2,512,128]{2,1,0:T(8,128)}, f32[512,128]{1,0:T(8,128)}, f32[768,128]{1,0:T(8,128)}) custom-call(f32[16,2,32,512]{3,2,1,0:T(8,128)} %child_ref.1, f32[16,8,128]{2,1,0:T(8,128)} %pivot_ref.1, f32[16,40,768]{2,1,0:T(8,128)} %update_ref.1), custom_call_target="tpu_custom_call" | custom-call | tf_op jit(solution)/shard_map/gather_fronts/pallas_call | solution.py:101
  32.0 0.0 copy-start
  32.0 16.1 %front_factor.1 = (f32[640,128]{1,0:T(8,128)}, f32[640,640]{1,0:T(8,128)}, f32[1,1,128]{2,1,0:T(1,128)}) custom-call(s32[16,2,512]{2,1,0:T(2,128)} %map_ref.1, f32[2,512,128]{2,1,0:T(8,128)} %get-tuple-element.13.near_ref, f32[2,512,128]{2,1,0:T(8,128)} %get-tuple-element.14.next_ref, f32[512,128]{1,0:T(8,128)} %get-tuple-element.15.far_ref, ...), custom_call_target="tpu_custom_call" | custom-call | tf_op jit(solution)/shard_map/front_factor/pallas_call | solution.py:250
  48.2 33.1 %scatter_fronts.1 = (f32[16,40,128]{2,1,0:T(8,128)}, f32[16,40,640]{2,1,0:T(8,128)}, f32[1,1]{1,0:T(1,128)}) custom-call(f32[640,128]{1,0:T(8,128)} %get-tuple-element.17.lhat_ref, f32[640,640]{1,0:T(8,128)} %get-tuple-element.18.rest_ref, f32[1,1,128]{2,1,0:T(1,128)} %get-tuple-element.19.negative_ref), custom_call_target="tpu_custom_call" | custom-call | tf_op jit(solution)/shard_map/scatter_fronts/pallas_call | solution.py:348
  81.3 0.0 copy-done
  81.3 0.0 copy-start.1
  81.3 2.8 %slice_add_fusion = f32[16,40,640]{2,1,0:T(8,128)} fusion(f32[16,40,640]{2,1,0:T(8,128)} %get-tuple-element.21, f32[16,40,768]{2,1,0:T(8,128)S(1)} %copy-done), kind=kLoop, calls=%fused_computation | loop fusion | flops 409600 | bytes 4915200 | tf_op jit(solution)/shard_map/add | solution.py:376
  84.1 0.0 copy-done.1
  84.1 0.7 copy.9
Async XLA Ops:
  32.0 49.3 %copy-start = (f32[16,40,768]{2,1,0:T(8,128)S(1)}, f32[16,40,768]{2,1,0:T(8,128)}, u32[]{:S(2)}) copy-start(f32[16,40,768]{2,1,0:T(8,128)} %update_ref.1) | copy-start | bytes 5898244
  81.3 2.8 %copy-start.1 = (f32[16,40,128]{2,1,0:T(8,128)S(1)}, f32[16,40,128]{2,1,0:T(8,128)}, u32[]{:S(2)}) copy-start(f32[16,40,128]{2,1,0:T(8,128)} %get-tuple-element.26) | copy-start | bytes 983044

commit v4 on v3

v4 whole, which is shorter than its diff:
```python
import jax
import jax.numpy as jnp
from jax import lax
from jax.experimental import pallas as pl
from jax.experimental.pallas import tpu as pltpu
from jax.sharding import PartitionSpec as P

MESH = pl.DeviceIdType.MESH
F32 = jnp.float32
BF16 = jnp.bfloat16
HIGHEST = lax.Precision.HIGHEST

N_ROW = 16
N_COL = 8
SIDE = 4
S = 128
CU = 512
U = 640
F = 768
SP = 8
UP = 40
HELD = 32
BLOCK = 32
OFFSETS = [
    (dx, (dx + turn) % SIDE)
    for turn in range(SIDE)
    for dx in range(SIDE)
    if (dx, (dx + turn) % SIDE) != (0, 0)
]
PEERS = len(OFFSETS)
PIECES = 7


def peer(me, dx, dz):
    x = lax.rem(me // SIDE + dx, SIDE)
    z = lax.rem(lax.rem(me, SIDE) + dz, SIDE)
    return x * SIDE + z


def to_row(source, target, send_sem, recv_sem, row):
    return pltpu.make_async_remote_copy(
        src_ref=source,
        dst_ref=target,
        send_sem=send_sem,
        recv_sem=recv_sem,
        device_id={"row": row},
        device_id_type=MESH,
    )


def split(values):
    high = values.astype(BF16)
    low = (values - high.astype(F32)).astype(BF16)
    return high, low


def nt_dot(a, b, precision=None):
    return lax.dot_general(
        a, b, (((1,), (1,)), ((), ())), precision=precision, preferred_element_type=F32
    )


def spread_lane(values, lane):
    return jnp.broadcast_to(values[:, lane : lane + 1], (8, 128))


def spread_row(values, row):
    return jnp.broadcast_to(values[row : row + 1, :], (8, 128))


def factor_in_place(work, meanwhile):
    sub = lax.broadcasted_iota(jnp.int32, (8, 128), 0)
    groups = BLOCK // 8
    for block in range(S // BLOCK):
        base = block * BLOCK
        left = [work[base + 8 * g : base + 8 * g + 8, 0:128] for g in range(groups)]
        right = [work[base + 8 * g : base + 8 * g + 8, 128:256] for g in range(groups)]
        for panel in range(groups):
            active = range(panel, groups)
            columns = [
                {g: spread_lane(left[g], base + 8 * panel + j) for g in active} for j in range(8)
            ]
            for j in range(8):
                scale = 1.0 / spread_row(columns[j][panel], j)
                row_left = spread_row(left[panel], j)
                row_right = spread_row(right[panel], j)
                across = {i: spread_row(columns[i][panel], j) for i in range(j + 1, 8)}
                for g in active:
                    multiplier = columns[j][g] * scale
                    if g == panel:
                        multiplier = jnp.where(sub > j, multiplier, 0.0)
                    for i in range(j + 1, 8):
                        columns[i][g] = columns[i][g] - multiplier * across[i]
                    left[g] = left[g] - multiplier * row_left
                    right[g] = right[g] - multiplier * row_right
            if meanwhile:
                meanwhile.pop(0)()
        strip_left = jnp.concatenate(left, axis=0)
        strip_right = jnp.concatenate(right, axis=0)
        work[base : base + BLOCK, 0:128] = strip_left
        work[base : base + BLOCK, 128:256] = strip_right
        after = base + BLOCK
        if after < S:
            lanes = lax.broadcasted_iota(jnp.int32, (BLOCK, 128), 1)
            places = lax.broadcasted_iota(jnp.int32, (BLOCK, 128), 0) + base
            diagonal = jnp.sum(
                jnp.where(lanes == places, strip_left, 0.0), axis=1, keepdims=True
            )
            lower = strip_left / diagonal
            strip = jnp.concatenate([strip_left, strip_right], axis=1)
            product = lax.dot_general(
                lower, strip, (((0,), (0,)), ((), ())), precision=HIGHEST, preferred_element_type=F32
            )
            work[after:S, :] = work[after:S, :] - product[after:S, :]
    while meanwhile:
        meanwhile.pop(0)()


def fronts_kernel(
    child_ref, pivot_ref, update_ref, map_ref, lhat_out, rest_out, share_out,
    maps, near_ref, next_ref, far_ref, panel_ref, hot_ref, high_ref, low_ref, spread_ref, work,
    lhat_ref, rest_ref, negative_ref, counts,
    own_sem, in_send, in_recv, out_send, out_recv, count_send, count_recv, row_send, row_recv,
):
    me = lax.axis_index("row")
    col = lax.axis_index("col")
    others = [peer(me, dx, dz) for dx, dz in OFFSETS]
    columns = [lax.rem(col + d, N_COL) for d in range(1, N_COL)]

    barrier = pltpu.get_barrier_semaphore()
    for other in others:
        pl.semaphore_signal(barrier, inc=1, device_id={"row": other}, device_id_type=MESH)
    for other in columns:
        pl.semaphore_signal(barrier, inc=1, device_id={"col": other}, device_id_type=MESH)

    group = me // SIDE
    near = pl.multiple_of(group * 128, 128)
    following = pl.multiple_of(lax.rem(group + 1, 4) * 128, 128)
    opposite = pl.multiple_of(lax.rem(group + 2, 4) * 128, 128)
    far_child = group // 2
    held = pl.ds(pl.multiple_of(me * HELD, HELD), HELD)
    pivot_rows = pl.ds(pl.multiple_of(me * SP, SP), SP)
    update_rows = pl.ds(pl.multiple_of(S + me * UP, SP), UP)

    def pieces(front):
        return (
            (pivot_ref.at[front], panel_ref.at[pivot_rows]),
            (child_ref.at[front, 0, :, pl.ds(near, 128)], near_ref.at[0, held]),
            (child_ref.at[front, 0, :, pl.ds(following, 128)], next_ref.at[0, held]),
            (child_ref.at[front, far_child, :, pl.ds(opposite, 128)], far_ref.at[held]),
            (child_ref.at[front, 1, :, pl.ds(near, 128)], near_ref.at[1, held]),
            (child_ref.at[front, 1, :, pl.ds(following, 128)], next_ref.at[1, held]),
            (update_ref.at[front, :, pl.ds(0, S)], panel_ref.at[update_rows]),
        )

    map_copy = pltpu.make_async_copy(map_ref.at[me], maps, own_sem.at[PIECES])
    map_copy.start()
    own = [
        pltpu.make_async_copy(source, target, own_sem.at[i])
        for i, (source, target) in enumerate(pieces(me))
    ]
    for copy in own:
        copy.start()
    pl.semaphore_wait(barrier, PEERS + N_COL - 1)
    incoming = [
        [
            to_row(*pieces(other)[i], in_send.at[place, i], in_recv.at[place, i], other)
            for place, other in enumerate(others)
        ]
        for i in range(PIECES)
    ]
    for kind in incoming:
        for copy in kind:
            copy.start()

    def arrived(kinds):
        for i in kinds:
            own[i].wait()
            for copy in incoming[i]:
                copy.wait_recv()

    map_copy.wait()
    for child in range(2):
        indices = maps[child : child + 1, :]
        position = lax.broadcasted_iota(jnp.int32, (F, CU), 0)
        hot_ref[child] = jnp.where(indices == position, 1.0, 0.0).astype(BF16)

    def fill(i, j, block):
        high, low = split(block)
        high_ref[128 * i : 128 * i + 128, 128 * j : 128 * j + 128] = high
        low_ref[128 * i : 128 * i + 128, 128 * j : 128 * j + 128] = low

    def spread_child(child):
        for i in range(4):
            rows = slice(128 * i, 128 * i + 128)
            fill(i, i, near_ref[child, rows, :])
            block = next_ref[child, rows, :]
            fill(i, (i + 1) % 4, block)
            fill((i + 1) % 4, i, block.T)
        for i in (2 * child, 2 * child + 1):
            block = far_ref[128 * i : 128 * i + 128, :]
            fill(i, (i + 2) % 4, block)
            fill((i + 2) % 4, i, block.T)
        for part, ref in enumerate((high_ref, low_ref)):
            spread_ref[child, part] = jnp.dot(
                hot_ref[child], ref[...], preferred_element_type=F32
            ).astype(BF16)

    def placed(start, size, first, count):
        total = None
        for child in range(2):
            hot = hot_ref[child, start : start + size, :]
            for part in range(2):
                term = nt_dot(spread_ref[child, part, first : first + count, :], hot)
                total = term if total is None else total + term
        return total

    arrived((0, 1, 2, 3))
    spread_child(0)
    arrived((4, 5))
    spread_child(1)
    early = placed(0, 256, 0, F)
    rest_ref[:, 0:128] = early[S:, 128:256]
    lane = lax.broadcasted_iota(jnp.int32, (S, S), 1)
    place = lax.broadcasted_iota(jnp.int32, (S, S), 0)
    work[:, 0:128] = panel_ref[0:S, :] + early[0:S, 0:128]
    work[:, 128:256] = jnp.where(lane == place, 1.0, 0.0)

    def later(start, first):
        def run():
            rest_ref[first : first + 160, start : start + 256] = placed(S + start, 256, S + first, 160)
        return run

    factor_in_place(work, [later(start, first) for start in (128, 384) for first in range(0, U, 160)])
    inverse = work[:, 128:256]
    pivots = jnp.sum(jnp.where(lane == place, work[:, 0:128], 0.0), axis=0, keepdims=True)
    negative = jnp.where(pivots < 0.0, 1.0, 0.0)
    negative_ref[0] = negative
    counts[me, pl.ds(col, 1)] = negative[None]
    tallies = []
    for i, other in enumerate(columns):
        tallies.append(
            pltpu.make_async_remote_copy(
                src_ref=negative_ref,
                dst_ref=counts.at[me, pl.ds(col, 1)],
                send_sem=count_send.at[i],
                recv_sem=count_recv.at[i],
                device_id={"col": other},
                device_id_type=MESH,
            )
        )
        tallies[-1].start()
    arrived((6,))
    lhat = nt_dot(panel_ref[S:, :] + early[S:, 0:128], inverse, HIGHEST)
    lhat_ref[...] = lhat

    def share(row):
        return pl.ds(pl.multiple_of(row * UP, SP), UP)

    outgoing = [
        [
            to_row(
                source.at[share(other)], target.at[me], out_send.at[i, kind], out_recv.at[i, kind], other
            )
            for i, other in enumerate(others)
        ]
        for kind, (source, target) in enumerate(((lhat_ref, lhat_out), (rest_ref, rest_out)))
    ]
    for copy in outgoing[0]:
        copy.start()
    scaled = lhat / pivots
    for start, size in ((0, 256), (256, 256), (512, 128)):
        correction = nt_dot(scaled, lhat[start : start + size], HIGHEST)
        rest_ref[:, start : start + size] = rest_ref[:, start : start + size] - correction
    for copy in tallies:
        copy.wait()
    forwards = [
        to_row(counts.at[me], counts.at[me], row_send.at[i], row_recv.at[i], other)
        for i, other in enumerate(others)
    ]
    for copy in forwards:
        copy.start()
    for copy in outgoing[1]:
        copy.start()
    lhat_out[me] = lhat_ref[share(me), :]
    rest_out[me] = rest_ref[share(me), :]
    for copy in forwards:
        copy.wait()
    total = counts[0]
    for row in range(1, N_ROW):
        total = total + counts[row]
    flat = jnp.sum(total, axis=0)
    share_out[...] = jnp.sum(flat, axis=1, keepdims=True) / float(N_ROW * N_COL * S)
    for kind in outgoing:
        for copy in kind:
            copy.wait()
    for kind in incoming:
        for copy in kind:
            copy.wait_send()


def fronts(child_blocks, front_pivot, front_update, child_map):
    any_spec = pl.BlockSpec(memory_space=pl.ANY)
    vmem_spec = pl.BlockSpec(memory_space=pltpu.VMEM)
    dma = pltpu.SemaphoreType.DMA
    return pl.pallas_call(
        fronts_kernel,
        out_shape=(
            jax.ShapeDtypeStruct((N_ROW, UP, S), F32),
            jax.ShapeDtypeStruct((N_ROW, UP, U), F32),
            jax.ShapeDtypeStruct((1, 1), F32),
        ),
        in_specs=[any_spec] * 4,
        out_specs=(vmem_spec,) * 3,
        scratch_shapes=[
            pltpu.VMEM((2, CU), jnp.int32),
            pltpu.VMEM((2, CU, 128), F32),
            pltpu.VMEM((2, CU, 128), F32),
            pltpu.VMEM((CU, 128), F32),
            pltpu.VMEM((F, S), F32),
            pltpu.VMEM((2, F, CU), BF16),
            pltpu.VMEM((CU, CU), BF16),
            pltpu.VMEM((CU, CU), BF16),
            pltpu.VMEM((2, 2, F, CU), BF16),
            pltpu.VMEM((S, 2 * S), F32),
            pltpu.VMEM((U, S), F32),
            pltpu.VMEM((U, U), F32),
            pltpu.VMEM((1, 1, S), F32),
            pltpu.VMEM((N_ROW, N_COL, 1, S), F32),
            dma((PIECES + 1,)),
            dma((PEERS, PIECES)),
            dma((PEERS, PIECES)),
            dma((PEERS, 2)),
            dma((PEERS, 2)),
            dma((N_COL - 1,)),
            dma((N_COL - 1,)),
            dma((PEERS,)),
            dma((PEERS,)),
        ],
        compiler_params=pltpu.CompilerParams(collective_id=0, has_side_effects=True),
        name="fronts",
    )(child_blocks, front_pivot, front_update, child_map)


def local(front_pivot, front_update, child_blocks, child_map):
    lhat, rest, share = fronts(child_blocks, front_pivot, front_update, child_map)
    return (lhat, front_update[:, :, S:] + rest, share[0, 0])


def solution(mesh):
    in_specs = (
        P("col", "row", None),
        P("col", "row", None),
        P("col", None, "row", None),
        P("col", None, None),
    )
    out_specs = (P("col", "row", None), P("col", "row", None), P())
    return jax.shard_map(local, mesh=mesh, in_specs=in_specs, out_specs=out_specs, check_vma=False)
```

time: 87.6 us -> 71 us (0.81)
  Pallas kernels: 80.6 us -> 64.8 us
    pallas_call x3 -> x1, Pallas kernels: 80.6 us -> 64.8 us  [fronts(): pl.pallas_call(fronts_kernel, out_shape=(jax.ShapeDtypeStruct((N_ROW, UP,...]
where the time goes in v4:
time: 71 us; the launch traced here: 70.8 us
  Pallas kernels  64.8 us (91%)
  other arithmetic  2.8 us (4%)
  between operations  2.43 us (3%)
  local copies, waits for them, and re-layouts  0.73 us (1%)
    pallas_call x1, Pallas kernels, fronts(): pl.pallas_call(fronts_kernel, out_shape=(jax.ShapeDtypeStruct((N_ROW, UP,...  64.8 us
    add x1, other arithmetic, local(): return (lhat, front_update[:, :, S:] + rest, share[0, 0])  2.8 us

profile of v4, /device:TPU:0, one launch (start us, length us, event | category | flops | bytes accessed | tf_op | source)
XLA Modules:
  0.0 70.8 jit_solution(11540171805209324267)
XLA Ops:
  0.6 0.0 copy-start
  0.6 64.8 %fronts.1 = (f32[16,40,128]{2,1,0:T(8,128)}, f32[16,40,640]{2,1,0:T(8,128)}, f32[1,1]{1,0:T(1,128)}) custom-call(f32[16,2,32,512]{3,2,1,0:T(8,128)} %child_ref.1, f32[16,8,128]{2,1,0:T(8,128)} %pivot_ref.1, f32[16,40,768]{2,1,0:T(8,128)} %update_ref.1, s32[16,2,512]{2,1,0:T(2,128)} %map_ref.1), custom_call_target="tpu_custom_call" | custom-call | tf_op jit(solution)/shard_map/fronts/pallas_call | solution.py:306
  65.5 0.0 copy-done
  65.5 0.0 copy-start.1
  65.5 2.8 %slice_add_fusion = f32[16,40,640]{2,1,0:T(8,128)} fusion(f32[16,40,640]{2,1,0:T(8,128)} %get-tuple-element.7, f32[16,40,768]{2,1,0:T(8,128)S(1)} %copy-done), kind=kLoop, calls=%fused_computation | loop fusion | flops 409600 | bytes 4915200 | tf_op jit(solution)/shard_map/add | solution.py:347
  68.3 0.0 copy-done.1
  68.3 0.7 %copy.9 = f32[16,40,128]{2,1,0:T(8,128)} copy(f32[16,40,128]{2,1,0:T(8,128)S(1)} %copy-done.1) | data formatting | bytes 655360
Async XLA Ops:
  0.6 64.9 %copy-start = (f32[16,40,768]{2,1,0:T(8,128)S(1)}, f32[16,40,768]{2,1,0:T(8,128)}, u32[]{:S(2)}) copy-start(f32[16,40,768]{2,1,0:T(8,128)} %update_ref.1) | copy-start | bytes 5898244
  65.5 2.8 %copy-start.1 = (f32[16,40,128]{2,1,0:T(8,128)S(1)}, f32[16,40,128]{2,1,0:T(8,128)}, u32[]{:S(2)}) copy-start(f32[16,40,128]{2,1,0:T(8,128)} %get-tuple-element.12) | copy-start | bytes 983044

commit v5 on v4

--- a/solution.py
+++ b/solution.py
@@ -93,7 +93,7 @@
                         columns[i][g] = columns[i][g] - multiplier * across[i]
                     left[g] = left[g] - multiplier * row_left
                     right[g] = right[g] - multiplier * row_right
-            if meanwhile:
+            if meanwhile and panel % 2 == 0:
                 meanwhile.pop(0)()
         strip_left = jnp.concatenate(left, axis=0)
         strip_right = jnp.concatenate(right, axis=0)
@@ -117,10 +117,10 @@
 
 
 def fronts_kernel(
-    child_ref, pivot_ref, update_ref, map_ref, lhat_out, rest_out, share_out,
+    child_ref, pivot_ref, update_ref, map_ref, lhat_out, schur_out, share_out,
     maps, near_ref, next_ref, far_ref, panel_ref, hot_ref, high_ref, low_ref, spread_ref, work,
-    lhat_ref, rest_ref, negative_ref, counts,
-    own_sem, in_send, in_recv, out_send, out_recv, count_send, count_recv, row_send, row_recv,
+    lhat_ref, rest_ref, added_ref, landed, trailing, negative_ref, counts,
+    own_sem, written_sem, in_send, in_recv, out_send, out_recv, count_send, count_recv, row_send, row_recv,
 ):
     me = lax.axis_index("row")
     col = lax.axis_index("col")
@@ -179,6 +179,10 @@
             for copy in incoming[i]:
                 copy.wait_recv()
 
+    trailing_copy = pltpu.make_async_copy(
+        update_ref.at[:, :, pl.ds(S, U)], trailing, own_sem.at[PIECES + 2]
+    )
+    trailing_copy.start()
     map_copy.wait()
     for child in range(2):
         indices = maps[child : child + 1, :]
@@ -190,7 +194,7 @@
         high_ref[128 * i : 128 * i + 128, 128 * j : 128 * j + 128] = high
         low_ref[128 * i : 128 * i + 128, 128 * j : 128 * j + 128] = low
 
-    def spread_child(child):
+    def fill_child(child):
         for i in range(4):
             rows = slice(128 * i, 128 * i + 128)
             fill(i, i, near_ref[child, rows, :])
@@ -201,9 +205,11 @@
             block = far_ref[128 * i : 128 * i + 128, :]
             fill(i, (i + 2) % 4, block)
             fill((i + 2) % 4, i, block.T)
+
+    def spread_rows(child, first, count):
         for part, ref in enumerate((high_ref, low_ref)):
-            spread_ref[child, part] = jnp.dot(
-                hot_ref[child], ref[...], preferred_element_type=F32
+            spread_ref[child, part, first : first + count, :] = jnp.dot(
+                hot_ref[child, first : first + count, :], ref[...], preferred_element_type=F32
             ).astype(BF16)
 
     def placed(start, size, first, count):
@@ -216,22 +222,36 @@
         return total
 
     arrived((0, 1, 2, 3))
-    spread_child(0)
+    fill_child(0)
+    spread_rows(0, 0, F)
     arrived((4, 5))
-    spread_child(1)
-    early = placed(0, 256, 0, F)
-    rest_ref[:, 0:128] = early[S:, 128:256]
+    fill_child(1)
+    spread_rows(1, 0, S)
     lane = lax.broadcasted_iota(jnp.int32, (S, S), 1)
     place = lax.broadcasted_iota(jnp.int32, (S, S), 0)
-    work[:, 0:128] = panel_ref[0:S, :] + early[0:S, 0:128]
+    work[:, 0:128] = panel_ref[0:S, :] + placed(0, S, 0, S)
     work[:, 128:256] = jnp.where(lane == place, 1.0, 0.0)
 
-    def later(start, first):
+    def spread_later(first):
+        return lambda: spread_rows(1, first, 320)
+
+    def placed_later(start, first):
         def run():
-            rest_ref[first : first + 160, start : start + 256] = placed(S + start, 256, S + first, 160)
+            block = placed(start, 256, first, 320)
+            rows = slice(first - S, first - S + 320)
+            if start == 0:
+                added_ref[rows, :] = block[:, 0:128]
+                rest_ref[rows, 0:128] = block[:, 128:256]
+            else:
+                rest_ref[rows, start - S : start - S + 256] = block
         return run
 
-    factor_in_place(work, [later(start, first) for start in (128, 384) for first in range(0, U, 160)])
+    halves = (S, S + 320)
+    factor_in_place(
+        work,
+        [spread_later(first) for first in halves]
+        + [placed_later(start, first) for start in (0, 256, 512) for first in halves],
+    )
     inverse = work[:, 128:256]
     pivots = jnp.sum(jnp.where(lane == place, work[:, 0:128], 0.0), axis=0, keepdims=True)
     negative = jnp.where(pivots < 0.0, 1.0, 0.0)
@@ -251,7 +271,7 @@
         )
         tallies[-1].start()
     arrived((6,))
-    lhat = nt_dot(panel_ref[S:, :] + early[S:, 0:128], inverse, HIGHEST)
+    lhat = nt_dot(panel_ref[S:, :] + added_ref[...], inverse, HIGHEST)
     lhat_ref[...] = lhat
 
     def share(row):
@@ -264,7 +284,7 @@
             )
             for i, other in enumerate(others)
         ]
-        for kind, (source, target) in enumerate(((lhat_ref, lhat_out), (rest_ref, rest_out)))
+        for kind, (source, target) in enumerate(((lhat_ref, lhat_out), (rest_ref, landed)))
     ]
     for copy in outgoing[0]:
         copy.start()
@@ -272,6 +292,10 @@
     for start, size in ((0, 256), (256, 256), (512, 128)):
         correction = nt_dot(scaled, lhat[start : start + size], HIGHEST)
         rest_ref[:, start : start + size] = rest_ref[:, start : start + size] - correction
+    for copy in outgoing[1]:
+        copy.start()
+    own_lhat = pltpu.make_async_copy(lhat_ref.at[share(me)], lhat_out.at[me], own_sem.at[PIECES + 1])
+    own_lhat.start()
     for copy in tallies:
         copy.wait()
     forwards = [
@@ -280,10 +304,17 @@
     ]
     for copy in forwards:
         copy.start()
-    for copy in outgoing[1]:
-        copy.start()
-    lhat_out[me] = lhat_ref[share(me), :]
-    rest_out[me] = rest_ref[share(me), :]
+    trailing_copy.wait()
+    written = [pltpu.make_async_copy(trailing.at[me], schur_out.at[me], written_sem.at[PEERS])]
+    trailing[me] = trailing[me] + rest_ref[share(me), :]
+    written[0].start()
+    for i, (dx, dz) in enumerate(OFFSETS):
+        outgoing[1][i].wait_recv()
+        source = peer(me, (SIDE - dx) % SIDE, (SIDE - dz) % SIDE)
+        trailing[source] = trailing[source] + landed[source]
+        copy = pltpu.make_async_copy(trailing.at[source], schur_out.at[source], written_sem.at[i])
+        copy.start()
+        written.append(copy)
     for copy in forwards:
         copy.wait()
     total = counts[0]
@@ -291,12 +322,16 @@
         total = total + counts[row]
     flat = jnp.sum(total, axis=0)
     share_out[...] = jnp.sum(flat, axis=1, keepdims=True) / float(N_ROW * N_COL * S)
-    for kind in outgoing:
-        for copy in kind:
-            copy.wait()
+    for copy in outgoing[0]:
+        copy.wait()
+    for copy in outgoing[1]:
+        copy.wait_send()
     for kind in incoming:
         for copy in kind:
             copy.wait_send()
+    own_lhat.wait()
+    for copy in written:
+        copy.wait()
 
 
 def fronts(child_blocks, front_pivot, front_update, child_map):
@@ -311,7 +346,7 @@
             jax.ShapeDtypeStruct((1, 1), F32),
         ),
         in_specs=[any_spec] * 4,
-        out_specs=(vmem_spec,) * 3,
+        out_specs=(any_spec, any_spec, vmem_spec),
         scratch_shapes=[
             pltpu.VMEM((2, CU), jnp.int32),
             pltpu.VMEM((2, CU, 128), F32),
@@ -325,9 +360,13 @@
             pltpu.VMEM((S, 2 * S), F32),
             pltpu.VMEM((U, S), F32),
             pltpu.VMEM((U, U), F32),
+            pltpu.VMEM((U, S), F32),
+            pltpu.VMEM((N_ROW, UP, U), F32),
+            pltpu.VMEM((N_ROW, UP, U), F32),
             pltpu.VMEM((1, 1, S), F32),
             pltpu.VMEM((N_ROW, N_COL, 1, S), F32),
-            dma((PIECES + 1,)),
+            dma((PIECES + 3,)),
+            dma((PEERS + 1,)),
             dma((PEERS, PIECES)),
             dma((PEERS, PIECES)),
             dma((PEERS, 2)),
@@ -343,8 +382,8 @@
 
 
 def local(front_pivot, front_update, child_blocks, child_map):
-    lhat, rest, share = fronts(child_blocks, front_pivot, front_update, child_map)
-    return (lhat, front_update[:, :, S:] + rest, share[0, 0])
+    lhat, schur, share = fronts(child_blocks, front_pivot, front_update, child_map)
+    return (lhat, schur, share[0, 0])
 
 
 def solution(mesh):

time: 71 us -> 67.4 us (0.949)
  Pallas kernels: 64.8 us -> 60.4 us
  local copies, waits for them, and re-layouts: 0.73 us -> 4.42 us
  other arithmetic: 2.8 us -> 0 us
    pallas_call x1, Pallas kernels: 64.8 us -> 60.4 us  [fronts(): pl.pallas_call(fronts_kernel, out_shape=(jax.ShapeDtypeStruct((N_ROW, UP,...]
    unnamed x5 -> x2, local copies, waits for them, and re-layouts: 0.73 us -> 4.42 us
    add x1 -> x0, other arithmetic: 2.8 us -> none  [local(): return (lhat, front_update[:, :, S:] + rest, share[0, 0])]
where the time goes in v5:
time: 67.4 us; the launch traced here: 67.2 us
  Pallas kernels  60.4 us (90%)
  local copies, waits for them, and re-layouts  4.42 us (7%)
  between operations  2.39 us (4%)
    pallas_call x1, Pallas kernels, fronts(): pl.pallas_call(fronts_kernel, out_shape=(jax.ShapeDtypeStruct((N_ROW, UP,...  60.4 us
    unnamed x2, local copies, waits for them, and re-layouts  4.42 us

profile of v5, /device:TPU:0, one launch (start us, length us, event | category | flops | bytes accessed | tf_op | source)
XLA Modules:
  0.0 67.2 jit_solution(3352259729042541769)
XLA Ops:
  0.6 60.4 %fronts.1 = (f32[16,40,128]{2,1,0:T(8,128)}, f32[16,40,640]{2,1,0:T(8,128)}, f32[1,1]{1,0:T(1,128)}) custom-call(f32[16,2,32,512]{3,2,1,0:T(8,128)} %child_ref.1, f32[16,8,128]{2,1,0:T(8,128)} %pivot_ref.1, f32[16,40,768]{2,1,0:T(8,128)} %update_ref.1, s32[16,2,512]{2,1,0:T(2,128)} %map_ref.1), custom_call_target="tpu_custom_call" | custom-call | tf_op jit(solution)/shard_map/fronts/pallas_call | solution.py:341
  61.0 1.7 %copy.10 = f32[16,40,128]{2,1,0:T(8,128)} copy(f32[16,40,128]{2,1,0:T(8,128)} %get-tuple-element.12) | data formatting | bytes 655360
  62.7 2.7 %copy.11 = f32[16,40,640]{2,1,0:T(8,128)} copy(f32[16,40,640]{2,1,0:T(8,128)} %get-tuple-element.13) | data formatting | bytes 3276800

commit v6 on v5

--- a/solution.py
+++ b/solution.py
@@ -20,13 +20,16 @@
 SP = 8
 UP = 40
 HELD = 32
-BLOCK = 32
-OFFSETS = [
-    (dx, (dx + turn) % SIDE)
-    for turn in range(SIDE)
-    for dx in range(SIDE)
-    if (dx, (dx + turn) % SIDE) != (0, 0)
-]
+BLOCK = 64
+OFFSETS = sorted(
+    [
+        (dx, (turn - dx) % SIDE)
+        for turn in range(SIDE)
+        for dx in range(SIDE)
+        if (dx, (turn - dx) % SIDE) != (0, 0)
+    ],
+    key=lambda offset: -sum(min(d, SIDE - d) for d in offset),
+)
 PEERS = len(OFFSETS)
 PIECES = 7
 
@@ -75,13 +78,16 @@
         base = block * BLOCK
         left = [work[base + 8 * g : base + 8 * g + 8, 0:128] for g in range(groups)]
         right = [work[base + 8 * g : base + 8 * g + 8, 128:256] for g in range(groups)]
+        inverted = []
         for panel in range(groups):
+            scales = jnp.zeros((8, 128), F32)
             active = range(panel, groups)
             columns = [
                 {g: spread_lane(left[g], base + 8 * panel + j) for g in active} for j in range(8)
             ]
             for j in range(8):
                 scale = 1.0 / spread_row(columns[j][panel], j)
+                scales = jnp.where(sub == j, scale, scales)
                 row_left = spread_row(left[panel], j)
                 row_right = spread_row(right[panel], j)
                 across = {i: spread_row(columns[i][panel], j) for i in range(j + 1, 8)}
@@ -93,6 +99,7 @@
                         columns[i][g] = columns[i][g] - multiplier * across[i]
                     left[g] = left[g] - multiplier * row_left
                     right[g] = right[g] - multiplier * row_right
+            inverted.append(scales)
             if meanwhile and panel % 2 == 0:
                 meanwhile.pop(0)()
         strip_left = jnp.concatenate(left, axis=0)
@@ -101,12 +108,7 @@
         work[base : base + BLOCK, 128:256] = strip_right
         after = base + BLOCK
         if after < S:
-            lanes = lax.broadcasted_iota(jnp.int32, (BLOCK, 128), 1)
-            places = lax.broadcasted_iota(jnp.int32, (BLOCK, 128), 0) + base
-            diagonal = jnp.sum(
-                jnp.where(lanes == places, strip_left, 0.0), axis=1, keepdims=True
-            )
-            lower = strip_left / diagonal
+            lower = strip_left * jnp.concatenate(inverted, axis=0)
             strip = jnp.concatenate([strip_left, strip_right], axis=1)
             product = lax.dot_general(
                 lower, strip, (((0,), (0,)), ((), ())), precision=HIGHEST, preferred_element_type=F32
@@ -119,8 +121,8 @@
 def fronts_kernel(
     child_ref, pivot_ref, update_ref, map_ref, lhat_out, schur_out, share_out,
     maps, near_ref, next_ref, far_ref, panel_ref, hot_ref, high_ref, low_ref, spread_ref, work,
-    lhat_ref, rest_ref, added_ref, landed, trailing, negative_ref, counts,
-    own_sem, written_sem, in_send, in_recv, out_send, out_recv, count_send, count_recv, row_send, row_recv,
+    lhat_ref, rest_ref, added_ref, landed, negative_ref, row_counts, total_ref, column_counts,
+    own_sem, in_send, in_recv, out_send, out_recv, count_send, count_recv, row_send, row_recv,
 ):
     me = lax.axis_index("row")
     col = lax.axis_index("col")
@@ -180,7 +182,7 @@
                 copy.wait_recv()
 
     trailing_copy = pltpu.make_async_copy(
-        update_ref.at[:, :, pl.ds(S, U)], trailing, own_sem.at[PIECES + 2]
+        update_ref.at[:, :, pl.ds(S, U)], schur_out, own_sem.at[PIECES + 1]
     )
     trailing_copy.start()
     map_copy.wait()
@@ -256,20 +258,13 @@
     pivots = jnp.sum(jnp.where(lane == place, work[:, 0:128], 0.0), axis=0, keepdims=True)
     negative = jnp.where(pivots < 0.0, 1.0, 0.0)
     negative_ref[0] = negative
-    counts[me, pl.ds(col, 1)] = negative[None]
-    tallies = []
-    for i, other in enumerate(columns):
-        tallies.append(
-            pltpu.make_async_remote_copy(
-                src_ref=negative_ref,
-                dst_ref=counts.at[me, pl.ds(col, 1)],
-                send_sem=count_send.at[i],
-                recv_sem=count_recv.at[i],
-                device_id={"col": other},
-                device_id_type=MESH,
-            )
-        )
-        tallies[-1].start()
+    row_counts[me] = negative
+    tallies = [
+        to_row(negative_ref.at[0], row_counts.at[me], row_send.at[i], row_recv.at[i], other)
+        for i, other in enumerate(others)
+    ]
+    for copy in tallies:
+        copy.start()
     arrived((6,))
     lhat = nt_dot(panel_ref[S:, :] + added_ref[...], inverse, HIGHEST)
     lhat_ref[...] = lhat
@@ -294,34 +289,36 @@
         rest_ref[:, start : start + size] = rest_ref[:, start : start + size] - correction
     for copy in outgoing[1]:
         copy.start()
-    own_lhat = pltpu.make_async_copy(lhat_ref.at[share(me)], lhat_out.at[me], own_sem.at[PIECES + 1])
-    own_lhat.start()
+    lhat_out[me] = lhat_ref[share(me), :]
     for copy in tallies:
         copy.wait()
+    row_total = jnp.sum(row_counts[...], axis=0)
+    total_ref[0] = row_total
+    column_counts[col] = row_total
+    trailing_copy.wait()
+    schur_out[me] = schur_out[me] + rest_ref[share(me), :]
     forwards = [
-        to_row(counts.at[me], counts.at[me], row_send.at[i], row_recv.at[i], other)
-        for i, other in enumerate(others)
+        pltpu.make_async_remote_copy(
+            src_ref=total_ref.at[0],
+            dst_ref=column_counts.at[col],
+            send_sem=count_send.at[i],
+            recv_sem=count_recv.at[i],
+            device_id={"col": other},
+            device_id_type=MESH,
+        )
+        for i, other in enumerate(columns)
     ]
     for copy in forwards:
         copy.start()
-    trailing_copy.wait()
-    written = [pltpu.make_async_copy(trailing.at[me], schur_out.at[me], written_sem.at[PEERS])]
-    trailing[me] = trailing[me] + rest_ref[share(me), :]
-    written[0].start()
     for i, (dx, dz) in enumerate(OFFSETS):
         outgoing[1][i].wait_recv()
         source = peer(me, (SIDE - dx) % SIDE, (SIDE - dz) % SIDE)
-        trailing[source] = trailing[source] + landed[source]
-        copy = pltpu.make_async_copy(trailing.at[source], schur_out.at[source], written_sem.at[i])
-        copy.start()
-        written.append(copy)
-    for copy in forwards:
-        copy.wait()
-    total = counts[0]
-    for row in range(1, N_ROW):
-        total = total + counts[row]
-    flat = jnp.sum(total, axis=0)
-    share_out[...] = jnp.sum(flat, axis=1, keepdims=True) / float(N_ROW * N_COL * S)
+        schur_out[source] = schur_out[source] + landed[source]
+        if i == PEERS // 2:
+            for copy in forwards:
+                copy.wait()
+            flat = jnp.sum(column_counts[...], axis=0)
+            share_out[...] = jnp.sum(flat, axis=1, keepdims=True) / float(N_ROW * N_COL * S)
     for copy in outgoing[0]:
         copy.wait()
     for copy in outgoing[1]:
@@ -329,9 +326,6 @@
     for kind in incoming:
         for copy in kind:
             copy.wait_send()
-    own_lhat.wait()
-    for copy in written:
-        copy.wait()
 
 
 def fronts(child_blocks, front_pivot, front_update, child_map):
@@ -341,12 +335,12 @@
     return pl.pallas_call(
         fronts_kernel,
         out_shape=(
-            jax.ShapeDtypeStruct((N_ROW, UP, S), F32),
-            jax.ShapeDtypeStruct((N_ROW, UP, U), F32),
+            pltpu.VMEM((N_ROW, UP, S), F32),
+            pltpu.VMEM((N_ROW, UP, U), F32),
             jax.ShapeDtypeStruct((1, 1), F32),
         ),
         in_specs=[any_spec] * 4,
-        out_specs=(any_spec, any_spec, vmem_spec),
+        out_specs=(vmem_spec, vmem_spec, vmem_spec),
         scratch_shapes=[
             pltpu.VMEM((2, CU), jnp.int32),
             pltpu.VMEM((2, CU, 128), F32),
@@ -362,11 +356,11 @@
             pltpu.VMEM((U, U), F32),
             pltpu.VMEM((U, S), F32),
             pltpu.VMEM((N_ROW, UP, U), F32),
-            pltpu.VMEM((N_ROW, UP, U), F32),
             pltpu.VMEM((1, 1, S), F32),
-            pltpu.VMEM((N_ROW, N_COL, 1, S), F32),
-            dma((PIECES + 3,)),
-            dma((PEERS + 1,)),
+            pltpu.VMEM((N_ROW, 1, S), F32),
+            pltpu.VMEM((1, 1, S), F32),
+            pltpu.VMEM((N_COL, 1, S), F32),
+            dma((PIECES + 2,)),
             dma((PEERS, PIECES)),
             dma((PEERS, PIECES)),
             dma((PEERS, 2)),
@@ -381,8 +375,36 @@
     )(child_blocks, front_pivot, front_update, child_map)
 
 
+def store_kernel(lhat_ref, schur_ref, lhat_out, schur_out, sem):
+    copies = [pltpu.make_async_copy(lhat_ref, lhat_out, sem.at[N_ROW])]
+    for i in range(N_ROW):
+        copies.append(pltpu.make_async_copy(schur_ref.at[i], schur_out.at[i], sem.at[i]))
+    for copy in copies:
+        copy.start()
+    for copy in copies:
+        copy.wait()
+
+
+def store(lhat, schur):
+    any_spec = pl.BlockSpec(memory_space=pl.ANY)
+    vmem_spec = pl.BlockSpec(memory_space=pltpu.VMEM)
+    return pl.pallas_call(
+        store_kernel,
+        out_shape=(
+            jax.ShapeDtypeStruct(lhat.shape, F32),
+            jax.ShapeDtypeStruct(schur.shape, F32),
+        ),
+        in_specs=[vmem_spec] * 2,
+        out_specs=(any_spec,) * 2,
+        scratch_shapes=[pltpu.SemaphoreType.DMA((N_ROW + 1,))],
+        compiler_params=pltpu.CompilerParams(vmem_limit_bytes=1 << 20),
+        name="store",
+    )(lhat, schur)
+
+
 def local(front_pivot, front_update, child_blocks, child_map):
     lhat, schur, share = fronts(child_blocks, front_pivot, front_update, child_map)
+    lhat, schur = store(lhat, schur)
     return (lhat, schur, share[0, 0])
 
 

time: 67.4 us -> 65.6 us (0.973)
  local copies, waits for them, and re-layouts: 4.42 us -> 0 us
  Pallas kernels: 60.4 us -> 62.3 us
    unnamed x2 -> x0, local copies, waits for them, and re-layouts: 4.42 us -> none
    pallas_call x1 -> x2, Pallas kernels: 60.4 us -> 62.3 us  [the longest x1 60.9 us: fronts(): pl.pallas_call(fronts_kernel, out_shape=(pltpu.VMEM((N_ROW, UP, S), F32),...]
where the time goes in v6:
time: 65.6 us; the launch traced here: 64.7 us
  Pallas kernels  62.3 us (95%)
  between operations  2.4 us (4%)
    pallas_call x1, Pallas kernels, fronts(): pl.pallas_call(fronts_kernel, out_shape=(pltpu.VMEM((N_ROW, UP, S), F32),...  60.9 us
    pallas_call x1, Pallas kernels, store(): pl.pallas_call(store_kernel, out_shape=(jax.ShapeDtypeStruct(lhat.shape,...  1.41 us

profile of v6, /device:TPU:0, one launch (start us, length us, event | category | flops | bytes accessed | tf_op | source)
XLA Modules:
  0.0 64.7 jit_solution(2475234554691994099)
XLA Ops:
  0.6 60.9 %fronts.1 = (f32[16,40,128]{2,1,0:T(8,128)S(1)}, f32[16,40,640]{2,1,0:T(8,128)S(1)}, f32[1,1]{1,0:T(1,128)}) custom-call(f32[16,2,32,512]{3,2,1,0:T(8,128)} %child_ref.1, f32[16,8,128]{2,1,0:T(8,128)} %pivot_ref.1, f32[16,40,768]{2,1,0:T(8,128)} %update_ref.1, s32[16,2,512]{2,1,0:T(2,128)} %map_ref.1), custom_call_target="tpu_custom_call" | custom-call | tf_op jit(solution)/shard_map/fronts/pallas_call | solution.py:335
  61.6 1.4 %store.1 = (f32[16,40,128]{2,1,0:T(8,128)}, f32[16,40,640]{2,1,0:T(8,128)}) custom-call(f32[16,40,128]{2,1,0:T(8,128)S(1)} %get-tuple-element.8.lhat_ref, f32[16,40,640]{2,1,0:T(8,128)S(1)} %get-tuple-element.9.schur_ref), custom_call_target="tpu_custom_call" | custom-call | tf_op jit(solution)/shard_map/store/pallas_call | solution.py:391

commit v7 on v6

--- a/solution.py
+++ b/solution.py
@@ -21,15 +21,8 @@
 UP = 40
 HELD = 32
 BLOCK = 64
-OFFSETS = sorted(
-    [
-        (dx, (turn - dx) % SIDE)
-        for turn in range(SIDE)
-        for dx in range(SIDE)
-        if (dx, (turn - dx) % SIDE) != (0, 0)
-    ],
-    key=lambda offset: -sum(min(d, SIDE - d) for d in offset),
-)
+ALL = [(dx, (dx + t) % 4) for t in range(4) for dx in range(4) if (dx, (dx + t) % 4) != (0, 0)]
+OFFSETS = ALL
 PEERS = len(OFFSETS)
 PIECES = 7
 

time: 65.6 us -> 62.8 us (0.957); the launches traced: 64.7 us -> 62.7 us
  Pallas kernels: 62.3 us -> 60.3 us
    pallas_call x1, Pallas kernels: 60.9 us -> 58.9 us  [fronts(): pl.pallas_call(fronts_kernel, out_shape=(pltpu.VMEM((N_ROW, UP, S), F32),...]
where the time goes in v7:
time: 62.8 us; the launch traced here: 62.7 us
  Pallas kernels  60.3 us (96%)
  between operations  2.4 us (4%)
    pallas_call x1, Pallas kernels, fronts(): pl.pallas_call(fronts_kernel, out_shape=(pltpu.VMEM((N_ROW, UP, S), F32),...  58.9 us
    pallas_call x1, Pallas kernels, store(): pl.pallas_call(store_kernel, out_shape=(jax.ShapeDtypeStruct(lhat.shape,...  1.41 us

profile of v7, /device:TPU:0, one launch (start us, length us, event | category | flops | bytes accessed | tf_op | source)
XLA Modules:
  0.0 62.7 jit_solution(16785814401945574057)
XLA Ops:
  0.6 58.9 %fronts.1 = (f32[16,40,128]{2,1,0:T(8,128)S(1)}, f32[16,40,640]{2,1,0:T(8,128)S(1)}, f32[1,1]{1,0:T(1,128)}) custom-call(f32[16,2,32,512]{3,2,1,0:T(8,128)} %child_ref.1, f32[16,8,128]{2,1,0:T(8,128)} %pivot_ref.1, f32[16,40,768]{2,1,0:T(8,128)} %update_ref.1, s32[16,2,512]{2,1,0:T(2,128)} %map_ref.1), custom_call_target="tpu_custom_call" | custom-call | tf_op jit(solution)/shard_map/fronts/pallas_call | solution.py:328
  59.5 1.4 %store.1 = (f32[16,40,128]{2,1,0:T(8,128)}, f32[16,40,640]{2,1,0:T(8,128)}) custom-call(f32[16,40,128]{2,1,0:T(8,128)S(1)} %get-tuple-element.8.lhat_ref, f32[16,40,640]{2,1,0:T(8,128)S(1)} %get-tuple-element.9.schur_ref), custom_call_target="tpu_custom_call" | custom-call | tf_op jit(solution)/shard_map/store/pallas_call | solution.py:384

commit v8 on v7

--- a/solution.py
+++ b/solution.py
@@ -111,9 +111,61 @@
         meanwhile.pop(0)()
 
 
+def turned(values, shift):
+    shift %= 128
+    if shift == 0:
+        return values
+    return jnp.concatenate([values[:, 128 - shift :], values[:, : 128 - shift]], axis=1)
+
+
+def pack(near_src, packed_src, extra_src, quarter):
+    which = jnp.full((HELD, 128), quarter, jnp.int32)
+    lane = lax.broadcasted_iota(jnp.int32, (HELD, 128), 1)
+
+    def one(front, carry):
+        aligned = []
+        for child in range(2):
+            strip = near_src[front, child]
+            result = strip
+            for q in range(1, 4):
+                result = jnp.where(which == q, turned(strip, -32 * q), result)
+            aligned.append(result)
+        packed_src[front] = jnp.where(lane < 64, aligned[0], turned(aligned[1], 64))
+        chosen = jnp.where(which < 2, aligned[0], aligned[1])
+        extra = turned(chosen[0:8], -64)
+        for q in range(1, 4):
+            moved = turned(chosen[8 * q : 8 * q + 8], 32 * q - 64)
+            extra = jnp.where(lane[0:8] // 32 == q, moved, extra)
+        extra_src[front] = extra
+        return carry
+
+    lax.fori_loop(0, N_ROW, one, 0)
+
+
+def unpack(near_ref, extra_ref, child, group):
+    lane = lax.broadcasted_iota(jnp.int32, (8, 128), 1) // 32
+    rows = []
+    for s in range(4):
+        source = 4 * group + s
+        strip = near_ref[32 * source : 32 * source + 32, :]
+        strip = turned(strip, 32 * s - 64 * child)
+        if s // 2 == child:
+            extra = extra_ref[8 * source : 8 * source + 8, :]
+            for q in range(4):
+                moved = turned(extra, 32 * ((s + 2) % 4) - 32 * q)
+                rows.append(jnp.where(lane == (s + 2) % 4, moved, strip[8 * q : 8 * q + 8]))
+        else:
+            rows.append(strip)
+    half = jnp.concatenate(rows, axis=0)
+    above = lax.broadcasted_iota(jnp.int32, (128, 128), 0) // 32
+    ahead = (lax.broadcasted_iota(jnp.int32, (128, 128), 1) // 32 - above + 4) % 4
+    kept = (ahead < 2) | ((ahead == 2) & (above // 2 == child))
+    return jnp.where(kept, half, half.T)
+
+
 def fronts_kernel(
     child_ref, pivot_ref, update_ref, map_ref, lhat_out, schur_out, share_out,
-    maps, near_ref, next_ref, far_ref, panel_ref, hot_ref, high_ref, low_ref, spread_ref, work,
+    maps, near_src, packed_src, extra_src, near_ref, extra_ref, next_ref, far_ref, panel_ref, hot_ref, high_ref, low_ref, spread_ref, work,
     lhat_ref, rest_ref, added_ref, landed, negative_ref, row_counts, total_ref, column_counts,
     own_sem, in_send, in_recv, out_send, out_recv, count_send, count_recv, row_send, row_recv,
 ):
@@ -137,23 +189,31 @@
     pivot_rows = pl.ds(pl.multiple_of(me * SP, SP), SP)
     update_rows = pl.ds(pl.multiple_of(S + me * UP, SP), UP)
 
+    extra_rows = pl.ds(pl.multiple_of(me * 8, 8), 8)
+
     def pieces(front):
         return (
             (pivot_ref.at[front], panel_ref.at[pivot_rows]),
-            (child_ref.at[front, 0, :, pl.ds(near, 128)], near_ref.at[0, held]),
+            (packed_src.at[front], near_ref.at[held]),
+            (extra_src.at[front], extra_ref.at[extra_rows]),
             (child_ref.at[front, 0, :, pl.ds(following, 128)], next_ref.at[0, held]),
             (child_ref.at[front, far_child, :, pl.ds(opposite, 128)], far_ref.at[held]),
-            (child_ref.at[front, 1, :, pl.ds(near, 128)], near_ref.at[1, held]),
             (child_ref.at[front, 1, :, pl.ds(following, 128)], next_ref.at[1, held]),
             (update_ref.at[front, :, pl.ds(0, S)], panel_ref.at[update_rows]),
         )
 
+    near_copy = pltpu.make_async_copy(
+        child_ref.at[:, :, :, pl.ds(near, 128)], near_src, own_sem.at[PIECES + 2]
+    )
+    near_copy.start()
     map_copy = pltpu.make_async_copy(map_ref.at[me], maps, own_sem.at[PIECES])
     map_copy.start()
     own = [
         pltpu.make_async_copy(source, target, own_sem.at[i])
         for i, (source, target) in enumerate(pieces(me))
     ]
+    near_copy.wait()
+    pack(near_src, packed_src, extra_src, lax.rem(me, 4))
     for copy in own:
         copy.start()
     pl.semaphore_wait(barrier, PEERS + N_COL - 1)
@@ -189,10 +249,13 @@
         high_ref[128 * i : 128 * i + 128, 128 * j : 128 * j + 128] = high
         low_ref[128 * i : 128 * i + 128, 128 * j : 128 * j + 128] = low
 
+    def fill_near(child):
+        for i in range(4):
+            fill(i, i, unpack(near_ref, extra_ref, child, i))
+
     def fill_child(child):
         for i in range(4):
             rows = slice(128 * i, 128 * i + 128)
-            fill(i, i, near_ref[child, rows, :])
             block = next_ref[child, rows, :]
             fill(i, (i + 1) % 4, block)
             fill((i + 1) % 4, i, block.T)
@@ -216,10 +279,12 @@
                 total = term if total is None else total + term
         return total
 
-    arrived((0, 1, 2, 3))
+    arrived((0, 1, 2, 3, 4))
+    fill_near(0)
     fill_child(0)
     spread_rows(0, 0, F)
-    arrived((4, 5))
+    fill_near(1)
+    arrived((5,))
     fill_child(1)
     spread_rows(1, 0, S)
     lane = lax.broadcasted_iota(jnp.int32, (S, S), 1)
@@ -336,7 +401,11 @@
         out_specs=(vmem_spec, vmem_spec, vmem_spec),
         scratch_shapes=[
             pltpu.VMEM((2, CU), jnp.int32),
-            pltpu.VMEM((2, CU, 128), F32),
+            pltpu.VMEM((N_ROW, 2, HELD, 128), F32),
+            pltpu.VMEM((N_ROW, HELD, 128), F32),
+            pltpu.VMEM((N_ROW, 8, 128), F32),
+            pltpu.VMEM((CU, 128), F32),
+            pltpu.VMEM((N_ROW * 8, 128), F32),
             pltpu.VMEM((2, CU, 128), F32),
             pltpu.VMEM((CU, 128), F32),
             pltpu.VMEM((F, S), F32),
@@ -353,7 +422,7 @@
             pltpu.VMEM((N_ROW, 1, S), F32),
             pltpu.VMEM((1, 1, S), F32),
             pltpu.VMEM((N_COL, 1, S), F32),
-            dma((PIECES + 2,)),
+            dma((PIECES + 3,)),
             dma((PEERS, PIECES)),
             dma((PEERS, PIECES)),
             dma((PEERS, 2)),

time: 62.8 us -> 61.2 us (0.975)
  Pallas kernels: 60.3 us -> 58.6 us
    pallas_call x1, Pallas kernels: 58.9 us -> 57.2 us  [fronts(): pl.pallas_call(fronts_kernel, out_shape=(pltpu.VMEM((N_ROW, UP, S), F32),...]
where the time goes in v8:
time: 61.2 us; the launch traced here: 61 us
  Pallas kernels  58.6 us (96%)
  between operations  2.4 us (4%)
    pallas_call x1, Pallas kernels, fronts(): pl.pallas_call(fronts_kernel, out_shape=(pltpu.VMEM((N_ROW, UP, S), F32),...  57.2 us
    pallas_call x1, Pallas kernels, store(): pl.pallas_call(store_kernel, out_shape=(jax.ShapeDtypeStruct(lhat.shape,...  1.41 us

profile of v8, /device:TPU:0, one launch (start us, length us, event | category | flops | bytes accessed | tf_op | source)
XLA Modules:
  0.0 61.0 jit_solution(399240830105055210)
XLA Ops:
  0.6 57.2 %fronts.1 = (f32[16,40,128]{2,1,0:T(8,128)S(1)}, f32[16,40,640]{2,1,0:T(8,128)S(1)}, f32[1,1]{1,0:T(1,128)}) custom-call(f32[16,2,32,512]{3,2,1,0:T(8,128)} %child_ref.1, f32[16,8,128]{2,1,0:T(8,128)} %pivot_ref.1, f32[16,40,768]{2,1,0:T(8,128)} %update_ref.1, s32[16,2,512]{2,1,0:T(2,128)} %map_ref.1), custom_call_target="tpu_custom_call" | custom-call | tf_op jit(solution)/shard_map/fronts/pallas_call | solution.py:393
  57.8 1.4 %store.1 = (f32[16,40,128]{2,1,0:T(8,128)}, f32[16,40,640]{2,1,0:T(8,128)}) custom-call(f32[16,40,128]{2,1,0:T(8,128)S(1)} %get-tuple-element.8.lhat_ref, f32[16,40,640]{2,1,0:T(8,128)S(1)} %get-tuple-element.9.schur_ref), custom_call_target="tpu_custom_call" | custom-call | tf_op jit(solution)/shard_map/store/pallas_call | solution.py:453

commit v9 on v8

--- a/solution.py
+++ b/solution.py
@@ -78,20 +78,36 @@
             columns = [
                 {g: spread_lane(left[g], base + 8 * panel + j) for g in active} for j in range(8)
             ]
-            for j in range(8):
-                scale = 1.0 / spread_row(columns[j][panel], j)
+            for j in range(0, 8, 2):
+                first, second = columns[j], columns[j + 1]
+                corner = spread_row(first[panel], j)
+                side = spread_row(first[panel], j + 1)
+                top = spread_row(second[panel], j)
+                determinant = corner * spread_row(second[panel], j + 1) - side * top
+                scale = 1.0 / corner
+                next_scale = corner * (1.0 / determinant)
+                ratio = side * scale
                 scales = jnp.where(sub == j, scale, scales)
+                scales = jnp.where(sub == j + 1, next_scale, scales)
                 row_left = spread_row(left[panel], j)
                 row_right = spread_row(right[panel], j)
-                across = {i: spread_row(columns[i][panel], j) for i in range(j + 1, 8)}
+                next_left = spread_row(left[panel], j + 1) - ratio * row_left
+                next_right = spread_row(right[panel], j + 1) - ratio * row_right
+                across = {i: spread_row(columns[i][panel], j) for i in range(j + 2, 8)}
+                next_across = {
+                    i: spread_row(columns[i][panel], j + 1) - ratio * across[i] for i in range(j + 2, 8)
+                }
                 for g in active:
-                    multiplier = columns[j][g] * scale
+                    multiplier = first[g] * scale
                     if g == panel:
                         multiplier = jnp.where(sub > j, multiplier, 0.0)
-                    for i in range(j + 1, 8):
-                        columns[i][g] = columns[i][g] - multiplier * across[i]
-                    left[g] = left[g] - multiplier * row_left
-                    right[g] = right[g] - multiplier * row_right
+                    next_multiplier = (second[g] - multiplier * top) * next_scale
+                    if g == panel:
+                        next_multiplier = jnp.where(sub > j + 1, next_multiplier, 0.0)
+                    for i in range(j + 2, 8):
+                        columns[i][g] = (columns[i][g] - multiplier * across[i]) - next_multiplier * next_across[i]
+                    left[g] = (left[g] - multiplier * row_left) - next_multiplier * next_left
+                    right[g] = (right[g] - multiplier * row_right) - next_multiplier * next_right
             inverted.append(scales)
             if meanwhile and panel % 2 == 0:
                 meanwhile.pop(0)()
@@ -341,9 +357,13 @@
     ]
     for copy in outgoing[0]:
         copy.start()
-    scaled = lhat / pivots
+    lhat_high, lhat_low = split(lhat)
+    scaled_high, scaled_low = split(lhat / pivots)
+    scaled_both = jnp.concatenate([scaled_high, scaled_low], axis=1)
+    lhat_twice = jnp.concatenate([lhat_high, lhat_high], axis=1)
     for start, size in ((0, 256), (256, 256), (512, 128)):
-        correction = nt_dot(scaled, lhat[start : start + size], HIGHEST)
+        part = slice(start, start + size)
+        correction = nt_dot(scaled_both, lhat_twice[part]) + nt_dot(scaled_high, lhat_low[part])
         rest_ref[:, start : start + size] = rest_ref[:, start : start + size] - correction
     for copy in outgoing[1]:
         copy.start()

time: 61.2 us -> 60.4 us (0.987)
  Pallas kernels: 58.6 us -> 57.9 us
    pallas_call x1, Pallas kernels: 57.2 us -> 56.5 us  [fronts(): pl.pallas_call(fronts_kernel, out_shape=(pltpu.VMEM((N_ROW, UP, S), F32),...]
where the time goes in v9:
time: 60.4 us; the launch traced here: 60.3 us
  Pallas kernels  57.9 us (96%)
  between operations  2.4 us (4%)
    pallas_call x1, Pallas kernels, fronts(): pl.pallas_call(fronts_kernel, out_shape=(pltpu.VMEM((N_ROW, UP, S), F32),...  56.5 us
    pallas_call x1, Pallas kernels, store(): pl.pallas_call(store_kernel, out_shape=(jax.ShapeDtypeStruct(lhat.shape,...  1.41 us

profile of v9, /device:TPU:0, one launch (start us, length us, event | category | flops | bytes accessed | tf_op | source)
XLA Modules:
  0.0 60.3 jit_solution(14643641872579899080)
XLA Ops:
  0.6 56.5 %fronts.1 = (f32[16,40,128]{2,1,0:T(8,128)S(1)}, f32[16,40,640]{2,1,0:T(8,128)S(1)}, f32[1,1]{1,0:T(1,128)}) custom-call(f32[16,2,32,512]{3,2,1,0:T(8,128)} %child_ref.1, f32[16,8,128]{2,1,0:T(8,128)} %pivot_ref.1, f32[16,40,768]{2,1,0:T(8,128)} %update_ref.1, s32[16,2,512]{2,1,0:T(2,128)} %map_ref.1), custom_call_target="tpu_custom_call" | custom-call | tf_op jit(solution)/shard_map/fronts/pallas_call | solution.py:413
  57.1 1.4 %store.1 = (f32[16,40,128]{2,1,0:T(8,128)}, f32[16,40,640]{2,1,0:T(8,128)}) custom-call(f32[16,40,128]{2,1,0:T(8,128)S(1)} %get-tuple-element.8.lhat_ref, f32[16,40,640]{2,1,0:T(8,128)S(1)} %get-tuple-element.9.schur_ref), custom_call_target="tpu_custom_call" | custom-call | tf_op jit(solution)/shard_map/store/pallas_call | solution.py:473
